TPU v7x, 32 devices: a whole 2x2x4 slice. The times are simulated.
32 devices in a mesh: fsdp: 8 (over z, y), ctx: 4 (over x, core).
Axes of the slice: x: 2, y: 2, z: 4, core: 2. Of those that a mesh axis runs over, the one named last changes fastest.
Arguments:
- tokens: bfloat16 [32768, 1024], P(('fsdp', 'ctx')), may hold values from -6 to 6
- valid_mask: int32 [32768], P(('fsdp', 'ctx')), may hold values from 0 to 1, as said below
- stretch_start: int32 [128], P(('fsdp', 'ctx')), may hold values from 0 to 1, as said below
- cotangent: bfloat16 [32768, 1024], P(('fsdp', 'ctx')), may hold values from -6 to 6
- norm_gain: float32 [1024], replicated, may hold values from 0.1 to 1.9
- in_weight: bfloat16 [1024, 4384], P(('fsdp', 'ctx')), may hold values from -0.1875 to 0.1875
- conv_weight: float32 [4, 2304], replicated, may hold values from -2 to 2
- conv_bias: float32 [2304], replicated, may hold values from -0.5 to 0.5
- step_bias: float32 [32], replicated, may hold values from -6 to -2
- decay_log: float32 [32], replicated, may hold values from -5 to 1.5
- skip_gain: float32 [32], replicated, may hold values from 0.5 to 1.5
- gate_gain: float32 [2048], replicated, may hold values from 0.1 to 1.9
- out_weight: bfloat16 [2048, 1024], P(('fsdp', 'ctx')), may hold values from -0.125 to 0.125
Outputs:
- output: bfloat16 [32768, 1024], P(('fsdp', 'ctx'))
- input_grad: float32 [32768, 1024], P(('fsdp', 'ctx'))
- in_weight_grad: float32 [1024, 4384], P(('fsdp', 'ctx'))
- out_weight_grad: float32 [2048, 1024], P(('fsdp', 'ctx'))
- norm_gain_grad: float32 [1024], replicated
- conv_weight_grad: float32 [4, 2304], replicated
- conv_bias_grad: float32 [2304], replicated
- step_bias_grad: float32 [32], replicated
- decay_log_grad: float32 [32], replicated
- skip_gain_grad: float32 [32], replicated
- gate_gain_grad: float32 [2048], replicated
Inputs may be any that keep to these rules, and one draw needn't show every extreme that they name: `stretch_start`: each group of 4096 tokens holds whole sequences laid end to end, each beginning at a stretch of 256 tokens; a sequence's first stretch lies a multiple of 4 stretches into its group, so the group's first stretch always begins one. A sequence's padding is only the tail of its last stretch; each sequence has 1024 tokens or more. `valid_mask`: 1 exactly for the tokens of sequences as described for stretch_start.
All inputs are finite; a program needn't handle non-finite values.
Results may differ from a plain program's by a relative error of at most 0.0092.
Values may be sent and summed in bfloat16 or wider, within the bound.
A program may use at most 320 MiB of HBM per device.

v0:
```python
import jax
import jax.numpy as jnp
from jax import lax
from jax.experimental import pallas as pl
from jax.experimental.pallas import tpu as pltpu
from jax.sharding import PartitionSpec as P

DI = 2048
HEADS = 32
P_SIZE = 64
N = 128
CONVK = 4
Q = 256
CH = 2304
DPROJ = 4384
UW = CH + 128
GW = 256
GROUPS = DI // GW
HALF = Q // 2

F32 = jnp.float32
BF16 = jnp.bfloat16
LOG2E = 1.4426950408889634
epsilon = 1e-05


def nn(a, b):
    return lax.dot_general(a, b, (((1,), (0,)), ((), ())), preferred_element_type=F32)


def nt(a, b):
    return lax.dot_general(a, b, (((1,), (1,)), ((), ())), preferred_element_type=F32)


def sigmoid(x):
    return 0.5 * jnp.tanh(0.5 * x) + 0.5


def softplus(x):
    e = jnp.exp(-jnp.abs(x))
    w = 1.0 + e
    d = w - 1.0
    return jnp.maximum(x, 0.0) + jnp.where(d == 0.0, e, jnp.log(w) * (e / jnp.where(d == 0.0, 1.0, d)))


def rows_of(shape):
    return lax.broadcasted_iota(jnp.int32, shape, 0)


def lanes_of(shape):
    return lax.broadcasted_iota(jnp.int32, shape, 1)


def split3(x):
    a = x.astype(BF16)
    r = x - a.astype(F32)
    b = r.astype(BF16)
    return a, b, (r - b.astype(F32)).astype(BF16)


def ordered_sum(triangle, x):
    a, b, c = split3(x)
    return nn(triangle, c) + nn(triangle, b) + nn(triangle, a)


def spread(x, out):
    out[0] = x
    for g in range(1, GROUPS):
        out[g] = pltpu.roll(x, 128 - 4 * g, 1)


def delayed(before, x, by):
    if by == 0:
        return x
    return pltpu.roll(jnp.concatenate([before, x], 0), by, 0)[8:]


def advanced(x, after, by):
    if by == 0:
        return x
    count = x.shape[0]
    return pltpu.roll(jnp.concatenate([x, after], 0), count + 8 - by, 0)[:count]


def fill_picks(out):
    for g in range(GROUPS):
        shape = (128, GW)
        head = lax.shift_right_logical(lanes_of(shape), 6) + 4 * g
        at = rows_of(shape)
        own = jnp.logical_and(jnp.bitwise_and(at, HEADS - 1) == head, at < 3 * HEADS)
        out[:, g * GW : (g + 1) * GW] = jnp.where(own, 1.0, 0.0).astype(BF16)


def in_parts(x):
    lane = lanes_of(x.shape)
    a, b, c = split3(jnp.where(lane < HEADS, x, 0.0))
    wide = a.astype(F32) + pltpu.roll(b.astype(F32), HEADS, 1) + pltpu.roll(c.astype(F32), 2 * HEADS, 1)
    return wide.astype(BF16)


def spread_rows(x, out):
    for g in range(GROUPS):
        out[g, 0:4] = x[4 * g : 4 * g + 4]


def head_lanes(x, i):
    return jnp.broadcast_to(x[:, i : i + 1], (x.shape[0], 128))


def pick_heads(g):
    shape = (GW, 128)
    return jnp.where(
        lax.shift_right_logical(rows_of(shape), 6) + 4 * g == lanes_of(shape), 1.0, 0.0
    ).astype(BF16)


def when_at(now, plan):
    plan = sorted(plan, key=lambda entry: entry[0])
    if len(plan) == 1:
        place, act = plan[0]

        @pl.when(now == place)
        def _():
            act()

    elif plan:
        middle = len(plan) // 2

        def early():
            when_at(now, plan[:middle])

        def late():
            when_at(now, plan[middle:])

        lax.cond(now < plan[middle][0], early, late)


def chain_peers():
    pos = lax.axis_index("ctx")
    return [(pos > 0, {"ctx": pos - 1}), (pos < lax.axis_size("ctx") - 1, {"ctx": pos + 1})]


def pass_on(message, arrived, sems, by):
    return pltpu.make_async_remote_copy(
        src_ref=message, dst_ref=arrived, send_sem=sems.at[0], recv_sem=sems.at[1],
        device_id={"ctx": lax.axis_index("ctx") + by}, device_id_type=pl.DeviceIdType.MESH,
    )


def forward_kernel(count, *refs):
    (
        u_ref, halo_ref, valid_ref, keep_ref, cw_ref, cb_ref, sb_ref, dl_ref, skip_ref,
    ) = refs[:9]
    own = refs[9 : 9 + count]
    (
        val_ref, vp_ref, conv_ref, bc_ref, ssd_ref, ent_ref, log_ref, step_ref, cum_ref, start_ref,
    ) = refs[9 + count : 19 + count]
    outs = refs[19 + count : 19 + 2 * count]
    (
        past, logs, picks, logt, inter, state, all_vp, all_val, all_bc, all_log, message, arrived, sems,
    ) = refs[19 + 2 * count : 32 + 2 * count]
    gather_sems = refs[32 + 2 * count :]
    i = pl.program_id(0)
    blocks = pl.num_programs(0) // 2
    first = i < blocks
    c = jnp.where(first, i, i - blocks)
    near = lax.axis_size("ctx")
    pos = lax.axis_index("ctx")
    plan = []
    if count:
        lists = [Gather(own[k], outs[k], *gather_sems[5 * k : 5 * k + 5]).steps() for k in range(count)]
        length = len(lists[0])
        for at in range(length + 2 * (count - 1)):
            acts = [lists[k][at - 2 * k] for k in range(count) if 0 <= at - 2 * k < length]
            plan.append((FORWARD_PLACES[at], lambda acts=acts: [act() for act in acts]))

    @pl.when(i == 0)
    def _():
        meet((box_peers() if count else []) + chain_peers())
        past[...] = halo_ref[:, :CH] * keep_ref[0, 0]
        fill_picks(picks)
        state[...] = jnp.zeros_like(state)
        cum_ref[...] = jnp.zeros_like(cum_ref)

    half = lanes_of((Q, 128)) < P_SIZE
    square = (Q, Q)
    causal = rows_of(square) >= lanes_of(square)

    @pl.when(first)
    def _():
        raw = u_ref[:, CH:] + sb_ref[...]
        step = softplus(raw) * valid_ref[...]
        step = jnp.where(lanes_of(step.shape) < HEADS, step, 0.0)
        rate = -jnp.exp(dl_ref[...]) * LOG2E
        logd = ordered_sum(jnp.where(causal, 1.0, 0.0).astype(BF16), step * rate)
        log_ref[...] = logd
        all_log[c] = logd
        step_ref[...] = step
        log_parts = in_parts(logd)
        step_parts = in_parts(step)

        def convolved(cols):
            x = u_ref[:, cols]
            before = past[:, cols]
            past[:, cols] = x[Q - 8 :]
            total = cb_ref[:, cols] + cw_ref[CONVK - 1 : CONVK, cols] * x
            for k in range(CONVK - 1):
                total = total + cw_ref[k : k + 1, cols] * delayed(before, x, CONVK - 1 - k)
            return total

        conv_b = convolved(pl.ds(DI, N))
        conv_c = convolved(pl.ds(DI + N, N))
        conv_ref[:, DI : DI + N] = conv_b.astype(BF16)
        conv_ref[:, DI + N :] = conv_c.astype(BF16)
        act_b = conv_b * sigmoid(conv_b)
        act_c = conv_c * sigmoid(conv_c)
        both = jnp.concatenate([act_b.astype(BF16), act_c.astype(BF16)], 1)
        bc_ref[...] = both
        all_bc[c] = both
        turned_b = act_b.T.astype(BF16)
        ent_ref[0] = state[...].astype(BF16)

        def group(g, unused):
            when_at(i * GROUPS + g, plan)
            wide = pl.ds(pl.multiple_of(g * GW, GW), GW)
            log_wide = nn(log_parts, picks[:, wide])
            step_wide = nn(step_parts, picks[:, wide])
            for j in range(2):
                cols = pl.ds(pl.multiple_of(g * GW + 128 * j, 128), 128)
                cv = convolved(cols)
                conv_ref[:, cols] = cv.astype(BF16)
                val = cv * sigmoid(cv)
                low = val.astype(BF16)
                val_ref[:, cols] = low
                all_val[c, :, cols] = low
                lp = log_wide[:, 128 * j : 128 * j + 128]
                vp = val * step_wide[:, 128 * j : 128 * j + 128]
                low = vp.astype(BF16)
                vp_ref[:, cols] = low
                all_vp[c, :, cols] = low
                last = lp[Q - 1 : Q, :]
                weighted = (vp * jnp.exp2(last - lp)).astype(BF16)
                state[:, cols] = jnp.exp2(last) * state[:, cols] + nn(turned_b, weighted)
                cum_ref[c + 1, :, cols] = cum_ref[c, :, cols] + last
            return unused

        lax.fori_loop(0, GROUPS, group, 0)

    for k in range(near):

        @pl.when(jnp.logical_and(i == blocks + k, pos == k))
        def _(k=k):
            if k:
                pass_on(message, arrived, sems, 1).wait_recv()
                entering = keep_ref[0, 0] * arrived[...].astype(F32)
                start_ref[...] = entering.astype(BF16)
            else:
                start_ref[...] = jnp.zeros_like(start_ref)
            if k < near - 1:
                if k:
                    message[...] = (jnp.exp2(cum_ref[blocks, 0:1, :]) * entering + state[...]).astype(BF16)
                else:
                    message[...] = state[...].astype(BF16)
                pass_on(message, arrived, sems, 1).start()

    @pl.when(jnp.logical_not(first))
    def _():
        logd = all_log[c]
        spread(logd, logs)
        spread_rows(logd.T, logt)
        inter[...] = jnp.where(causal, nt(all_bc[c, :, N:], all_bc[c, :, :N]), 0.0)
        left = jnp.where(half[:1], 1.0, 0.0).astype(BF16)
        right = jnp.where(half[:1], 0.0, 1.0).astype(BF16)

        def group(g, unused):
            when_at(i * GROUPS + g, plan)
            lg = logs[g]
            for j in range(2):
                cols = pl.ds(pl.multiple_of(g * GW + 128 * j, 128), 128)
                vp = all_vp[c, :, cols]
                v0 = vp * left
                v1 = vp * right
                top = []
                low = []
                for h in range(2):
                    row = logt[g, 2 * j + h : 2 * j + h + 1]
                    early, late = row[:, :HALF], row[:, HALF:]
                    lb = head_lanes(lg, 2 * j + h)
                    up, down = lb[:HALF], lb[HALF:]
                    top.append((inter[:HALF, :HALF] * jnp.exp2(jnp.minimum(up - early, 0.0))).astype(BF16))
                    low.append((inter[HALF:, :HALF] * jnp.exp2(jnp.minimum(down - early, 0.0))).astype(BF16))
                    low.append((inter[HALF:, HALF:] * jnp.exp2(jnp.minimum(down - late, 0.0))).astype(BF16))
                skipped = skip_ref[:, cols] * all_val[c, :, cols].astype(F32)
                above = nn(jnp.concatenate(top, 1), jnp.concatenate([v0[:HALF], v1[:HALF]], 0))
                below = nn(jnp.concatenate(low, 1), jnp.concatenate([v0, v1], 0))
                ssd_ref[:HALF, cols] = (above + skipped[:HALF]).astype(BF16)
                ssd_ref[HALF:, cols] = (below + skipped[HALF:]).astype(BF16)
            return unused

        lax.fori_loop(0, GROUPS, group, 0)

    @pl.when(jnp.logical_and(i == 2 * blocks - 1, pos < near - 1))
    def _():
        pass_on(message, arrived, sems, 1).wait_send()


def gate_kernel(
    start_ref, ssd_in, ent_ref, z_ref, val_ref, bc_ref, log_ref, cum_ref,
    tok_ref, cot_ref, valid_ref, ow_ref, gain_ref,
    out_ref, gated_ref, bg_ref, ds_ref, dz_ref, entt_ref, gnext_ref, gout_ref, dlp_ref, dc_ref, sums_ref,
    start, gstate, picks, ssd_s, mix_s, el_s, pe_s, gg_s, acc,
):
    i = pl.program_id(0)
    c = pl.num_programs(0) - 1 - i

    @pl.when(i == 0)
    def _():
        start[...] = start_ref[...].astype(F32)
        fill_picks(picks)
        gstate[...] = jnp.zeros_like(gstate)
        sums_ref[...] = jnp.zeros_like(sums_ref)

    log_parts = in_parts(log_ref[...])
    low_c = bc_ref[:, N:]
    turned_c = low_c.astype(F32).T.astype(BF16)
    acc[...] = jnp.zeros_like(acc)

    def enter(g, unused):
        cols = pl.ds(pl.multiple_of(g * GW, GW), GW)
        decay = jnp.exp2(nn(log_parts, picks[:, cols]))
        entering = (
            ent_ref[0, :, cols].astype(F32) + jnp.exp2(cum_ref[c, 0:1, cols]) * start[:, cols]
        ).astype(BF16)
        entt_ref[0, :, cols] = entering
        part = nn(low_c, entering)
        for j in range(2):
            pc = pl.ds(pl.multiple_of(g * GW + 128 * j, 128), 128)
            el = decay[:, 128 * j : 128 * j + 128]
            pe = el * part[:, 128 * j : 128 * j + 128]
            el_s[:, pc] = el
            pe_s[:, pc] = pe
            ssd = ssd_in[:, pc].astype(F32) + pe
            z = z_ref[:, pc].astype(F32)
            mixed = ssd * (z * sigmoid(z))
            ssd_s[:, pc] = ssd
            mix_s[:, pc] = mixed
            acc[...] += mixed * mixed
        return unused

    lax.fori_loop(0, GROUPS, enter, 0)
    inv = lax.rsqrt(jnp.sum(acc[...], axis=1, keepdims=True) * (1.0 / DI) + epsilon)
    inv = jnp.broadcast_to(inv, (Q, 128))
    valid = valid_ref[...]
    valid8 = jnp.concatenate([valid] * (tok_ref.shape[1] // 128), 1)
    branch_grad = (cot_ref[...].astype(F32) * valid8).astype(BF16)
    bg_ref[...] = branch_grad
    acc[...] = jnp.zeros_like(acc)

    def gate(g, unused):
        cols = pl.ds(pl.multiple_of(g * GW, GW), GW)
        ggrad = nt(branch_grad, ow_ref[cols, :])
        for j in range(2):
            pc = pl.ds(pl.multiple_of(g * GW + 128 * j, 128), 128)
            hat = mix_s[:, pc] * inv
            gain = gain_ref[:, pc]
            mix_s[:, pc] = hat
            gated_ref[:, pc] = (hat * gain).astype(BF16)
            gg = ggrad[:, 128 * j : 128 * j + 128]
            both = gg * hat
            sums_ref[0:1, pc] += jnp.sum(both, axis=0, keepdims=True)
            acc[...] += both * gain
            gg_s[:, pc] = gg * gain
        return unused

    lax.fori_loop(0, GROUPS, gate, 0)
    mean = jnp.sum(acc[...], axis=1, keepdims=True) * (1.0 / DI)
    mean = jnp.broadcast_to(mean, (Q, 128))

    for n in range(tok_ref.shape[1] // 256):
        cols = slice(256 * n, 256 * n + 256)
        branch = nn(gated_ref[...], ow_ref[:, cols])
        out_ref[:, cols] = (tok_ref[:, cols].astype(F32) + valid8[:, :256] * branch).astype(BF16)

    acc[...] = jnp.zeros_like(acc)
    dc_ref[...] = jnp.zeros_like(dc_ref)

    def back(g, unused):
        cols = pl.ds(pl.multiple_of(g * GW, GW), GW)
        dparts = []
        prods = []
        for j in range(2):
            pc = pl.ds(pl.multiple_of(g * GW + 128 * j, 128), 128)
            dmixed = inv * (gg_s[:, pc] - mix_s[:, pc] * mean)
            z = z_ref[:, pc].astype(F32)
            s = sigmoid(z)
            ds = (dmixed * (z * s)).astype(BF16)
            ds_ref[:, pc] = ds
            dz_ref[:, pc] = (dmixed * ssd_s[:, pc] * (s * (1.0 + z * (1.0 - s)))).astype(BF16)
            ds = ds.astype(F32)
            sums_ref[1:2, pc] += jnp.sum(ds * val_ref[:, pc].astype(F32), axis=0, keepdims=True)
            dparts.append((ds * el_s[:, pc]).astype(BF16))
            prods.append((ds * pe_s[:, pc]).astype(BF16))
        dpart = jnp.concatenate(dparts, 1)
        acc[...] += nn(jnp.concatenate(prods, 1), pick_heads(g))
        dc_ref[...] += nt(dpart, entt_ref[0, :, cols])
        gnext_ref[0, :, cols] = gstate[:, cols].astype(BF16)
        total = cum_ref[c + 1, 0:1, cols] - cum_ref[c, 0:1, cols]
        gstate[:, cols] = nn(turned_c, dpart) + jnp.exp2(total) * gstate[:, cols]
        return unused

    lax.fori_loop(0, GROUPS, back, 0)
    dlp_ref[...] = acc[...]

    @pl.when(c == 0)
    def _():
        gout_ref[...] = gstate[...].astype(BF16)


FORWARD_PLACES = tuple(5 * k for k in range(13))
MIXING_PLACES = (0, 5, 12, 31)
LINE_PLACES = (1, 4, 8, 12)
BACK_PLACES = (0, 4, 9, 19, 22, 25, 28, 31)


def acting(places, acts):
    joined = {}
    for place, act in zip(places, acts):
        joined.setdefault(place, []).append(act)
    return [(place, lambda acts=acts: [act() for act in acts]) for place, acts in joined.items()]


def plane_scratch(rows, columns):
    dma = pltpu.SemaphoreType.DMA
    return scatter_scratch(rows, columns)[:6] + [dma((4,))] * 4


def line_scratch(rows, columns):
    dma = pltpu.SemaphoreType.DMA
    return [pltpu.VMEM((1, LINE, rows, columns), BF16)] + [pltpu.VMEM((LINE, rows, columns), BF16)] * 2 + [
        dma((2, LINE))
    ] * 2


def mixing_kernel(count, *refs):
    ds_ref, vp_ref, bc_ref, log_ref, keep_ref, gout_ref, cum_ref = refs[:7]
    parts = refs[7 : 7 + count]
    dvp_ref, dbc_ref, dlt_ref, gin_ref = refs[7 + count : 11 + count]
    outs = refs[11 + count : 11 + 2 * count]
    (
        logs, logt, inter, dinter, rowsum, turned, colsum, message, arrived, sems,
    ) = refs[11 + 2 * count : 21 + 2 * count]
    i = pl.program_id(0)
    blocks = pl.num_programs(0)
    near = lax.axis_size("ctx")
    pos = lax.axis_index("ctx")
    plan = []
    if count:
        held = refs[21 + 2 * count :]
        part = Scatter(parts[0], None, *held[:6], None, None, tuple(held[6:10]) + (None, None))
        acts = [part.begin, part.corners, part.sides_out, lambda: part.hand_on(outs[0])]
        plan = acting(MIXING_PLACES, acts)

    @pl.when(i == 0)
    def _():
        meet((box_peers() if count else []) + chain_peers())

    for k in range(near):

        @pl.when(jnp.logical_and(i == k, pos == near - 1 - k))
        def _(k=k):
            total = gout_ref[...].astype(F32)
            if k:
                pass_on(message, arrived, sems, -1).wait_recv()
                gin_ref[...] = arrived[...]
                total = total + jnp.exp2(cum_ref[blocks, 0:1, :]) * arrived[...].astype(F32)
            else:
                gin_ref[...] = jnp.zeros_like(gin_ref)
            if k < near - 1:
                message[...] = (keep_ref[0, 0] * total).astype(BF16)
                pass_on(message, arrived, sems, -1).start()

    @pl.when(jnp.logical_and(i == blocks - 1, pos > 0))
    def _():
        pass_on(message, arrived, sems, -1).wait_send()

    logd = log_ref[...]
    spread(logd, logs)
    spread_rows(logd.T, logt)
    low_b = bc_ref[:, :N]
    low_c = bc_ref[:, N:]
    square = (Q, Q)
    causal = rows_of(square) <= lanes_of(square)
    inter[...] = jnp.where(causal, nt(low_b, low_c), 0.0)
    dinter[...] = jnp.zeros_like(dinter)
    half = lanes_of((Q, 128)) < P_SIZE
    lane = lanes_of((HALF, 128))

    def group(g, unused):
        when_at(i * GROUPS + g, plan)
        lg = logs[g]
        first_col = jnp.zeros((HALF, 128), F32)
        second_col = jnp.zeros((HALF, 128), F32)
        for j in range(2):
            cols = pl.ds(pl.multiple_of(g * GW + 128 * j, 128), 128)
            vp = vp_ref[:, cols].astype(F32)
            ds = ds_ref[:, cols]
            wide = ds.astype(F32)
            first = []
            second = []
            outs = []
            for h in range(2):
                head = 2 * j + h
                own = half if h == 0 else jnp.logical_not(half)
                vm = jnp.where(own, vp, 0.0).astype(BF16)
                dsm = jnp.where(own, wide, 0.0).astype(BF16)
                outs.append(dsm)
                row = logt[g, head : head + 1]
                early, late = row[:, :HALF], row[:, HALF:]
                lb = head_lanes(lg, head)
                up, down = lb[:HALF], lb[HALF:]
                dup = nt(vm[:HALF], ds)
                ddown = nt(vm[HALF:], ds[HALF:])
                decay = jnp.exp2(jnp.minimum(early - up, 0.0))
                grad = dup[:, :HALF] * decay
                dinter[:HALF, :HALF] += grad
                part = inter[:HALF, :HALF]
                first.append((part * decay).astype(BF16))
                both = grad * part
                row_early = jnp.sum(both, axis=0, keepdims=True)
                col = both
                decay = jnp.exp2(jnp.minimum(late - up, 0.0))
                grad = dup[:, HALF:] * decay
                dinter[:HALF, HALF:] += grad
                part = inter[:HALF, HALF:]
                first.append((part * decay).astype(BF16))
                both = grad * part
                row_late = jnp.sum(both, axis=0, keepdims=True)
                col = jnp.sum(col + both, axis=1, keepdims=True)
                first_col = jnp.where(lane == head, col, first_col)
                decay = jnp.exp2(jnp.minimum(late - down, 0.0))
                grad = ddown * decay
                dinter[HALF:, HALF:] += grad
                part = inter[HALF:, HALF:]
                second.append((part * decay).astype(BF16))
                both = grad * part
                row_late = row_late + jnp.sum(both, axis=0, keepdims=True)
                col = jnp.sum(both, axis=1, keepdims=True)
                second_col = jnp.where(lane == head, col, second_col)
                rowsum[g, head : head + 1, :HALF] = row_early
                rowsum[g, head : head + 1, HALF:] = row_late
            dvp_ref[:HALF, cols] = nn(
                jnp.concatenate(first, 1), jnp.concatenate(outs, 0)
            ).astype(BF16)
            dvp_ref[HALF:, cols] = nn(
                jnp.concatenate(second, 1), jnp.concatenate([outs[0][HALF:], outs[1][HALF:]], 0)
            ).astype(BF16)
        colsum[g, :HALF] = first_col
        colsum[g, HALF:] = second_col
        return unused

    lax.fori_loop(0, GROUPS, group, 0)
    turned[...] = jnp.zeros_like(turned)
    for g in range(GROUPS):
        turned[4 * g : 4 * g + 4] = rowsum[g, 0:4]
    total = turned[...].T
    for g in range(GROUPS):
        total = total - (colsum[g] if g == 0 else pltpu.roll(colsum[g], 4 * g, 1))
    dlt_ref[...] = total
    masked = jnp.where(causal, dinter[...], 0.0)
    dbc_ref[:, :N] = nn(masked.astype(BF16), low_c)
    dbc_ref[:, N:] = nn(masked.T.astype(BF16), low_b)


def back_kernel(count, *refs):
    (
        keep_ref, gin_ref, gnext_ref, entt_ref, cum_ref, vp_ref, val_ref, dvp_ref, ds_ref, conv_ref,
        u_ref, halo_ref, bc_ref, log_ref, step_ref, valid_ref, dlp_ref, dlt_ref, dbc_ref, dc_ref,
        cw_ref, sb_ref, dl_ref, skip_ref,
    ) = refs[:24]
    parts = refs[24 : 24 + count]
    du_ref, last_ref, edge_ref, sums_ref, small_ref = refs[24 + count : 29 + count]
    outs = refs[29 + count : 29 + 2 * count]
    gin, picks, head, epad, dlw, dst, drow = refs[29 + 2 * count : 36 + 2 * count]
    plan = []
    if count:
        held = refs[36 + 2 * count :]
        full = Scatter(parts[1], outs[1], *held[:8], held[8:14])
        line = Scatter(None, outs[0], None, held[14], None, None, None, None, *held[15:17], (None,) * 4 + tuple(held[17:19]))
        acts = [lambda: line.line(3), lambda: line.line(2), lambda: line.line(1), line.line_done]
        plan = acting(BACK_PLACES + LINE_PLACES, full.steps() + acts)
    i = pl.program_id(0)
    top = pl.num_programs(0)
    c = top - 1 - i

    @pl.when(i == 0)
    def _():
        if count:
            meet(box_peers())
            line.kept[0] = parts[0][...]
        gin[...] = gin_ref[...].astype(F32)
        fill_picks(picks)
        head[...] = jnp.zeros_like(head)
        sums_ref[...] = jnp.zeros_like(sums_ref)
        small_ref[...] = jnp.zeros_like(small_ref)

    log_parts = in_parts(log_ref[...])
    step_parts = in_parts(step_ref[...])
    low_b = bc_ref[:, :N]
    dlw[...] = jnp.zeros_like(dlw)
    dst[...] = jnp.zeros_like(dst)
    drow[...] = jnp.zeros_like(drow)

    def conv_back(cols, dact):
        cv = conv_ref[:, cols].astype(F32)
        s = sigmoid(cv)
        dcv = dact * (s * (1.0 + cv * (1.0 - s)))
        after = head[:, cols]
        head[:, cols] = dcv[:8]
        x = u_ref[:, cols]
        sums_ref[4:5, cols] += jnp.sum(dcv, axis=0, keepdims=True)
        total = None
        for j in range(CONVK):
            k = CONVK - 1 - j
            moved = advanced(dcv, after, j)
            sums_ref[k : k + 1, cols] += jnp.sum(moved * x, axis=0, keepdims=True)
            term = cw_ref[k : k + 1, cols] * moved
            total = term if total is None else total + term
        du_ref[:, cols] = total.astype(BF16)

        @pl.when(i == 0)
        def _():
            last_ref[:, cols] = total[Q - 8 :]

    def group(g, db):
        when_at(i * GROUPS + g, plan)
        cols = pl.ds(pl.multiple_of(g * GW, GW), GW)
        log_wide = nn(log_parts, picks[:, cols])
        step_wide = nn(step_parts, picks[:, cols])
        done = cum_ref[c + 1, 0:1, cols]
        after = jnp.exp2(cum_ref[top, 0:1, cols] - done)
        grad = gnext_ref[0, :, cols].astype(F32) + after * gin[:, cols]
        low_g = grad.astype(BF16)
        decay = jnp.exp2(done - cum_ref[c, 0:1, cols])
        row = decay * jnp.sum(grad * entt_ref[0, :, cols].astype(F32), axis=0, keepdims=True)
        coarse = row.astype(BF16).astype(F32)
        r = rows_of((16, GW))
        two = jnp.where(r == 0, jnp.broadcast_to(coarse, (16, GW)), 0.0)
        two = jnp.where(r == 1, jnp.broadcast_to(row - coarse, (16, GW)), two)
        chosen = pick_heads(g)
        drow[...] += nn(two.astype(BF16), chosen)
        dweighted = nn(low_b, low_g)
        weights = []
        moves = []
        stepped = []
        dacts = []
        for j in range(2):
            pc = pl.ds(pl.multiple_of(g * GW + 128 * j, 128), 128)
            lp = log_wide[:, 128 * j : 128 * j + 128]
            sp = step_wide[:, 128 * j : 128 * j + 128]
            fade = jnp.exp2(lp[Q - 1 : Q, :] - lp)
            vp = vp_ref[:, pc].astype(F32)
            faded = dweighted[:, 128 * j : 128 * j + 128] * fade
            weights.append((vp * fade).astype(BF16))
            moves.append((faded * vp).astype(BF16))
            both = dvp_ref[:, pc].astype(F32) + faded
            stepped.append((both * val_ref[:, pc].astype(F32)).astype(BF16))
            dacts.append((pc, sp * both + skip_ref[:, pc] * ds_ref[:, pc].astype(F32)))
        dlw[...] += nn(jnp.concatenate(moves, 1), chosen)
        dst[...] += nn(jnp.concatenate(stepped, 1), chosen)
        for pc, dact in dacts:
            conv_back(pc, dact)
        return db + nt(jnp.concatenate(weights, 1), low_g)

    db = lax.fori_loop(0, GROUPS, group, dbc_ref[:, :N])
    conv_back(pl.ds(DI, N), db)
    conv_back(pl.ds(DI + N, N), dbc_ref[:, N:] + dc_ref[...])

    moved = dlw[...]
    at_last = jnp.sum(moved, axis=0, keepdims=True) + drow[0:1] + drow[1:2]
    dlog = dlp_ref[...] + dlt_ref[...] - moved
    dlog = dlog + jnp.where(rows_of(dlog.shape) == Q - 1, at_last, 0.0)
    square = (Q, Q)
    later = jnp.where(rows_of(square) <= lanes_of(square), 1.0, 0.0).astype(BF16)
    dsum = ordered_sum(later, dlog)
    rate = -jnp.exp(dl_ref[...])
    dstep = (dst[...] + dsum * rate) * valid_ref[...]
    raw = u_ref[:, CH:] + sb_ref[...]
    draw = dstep * (1.0 / (1.0 + jnp.exp(-raw)))
    draw = jnp.where(lanes_of(draw.shape) < HEADS, draw, 0.0)
    du_ref[:, CH:] = draw.astype(BF16)
    small_ref[0:1] += jnp.sum(draw, axis=0, keepdims=True)
    small_ref[1:2] += jnp.sum(dsum * step_ref[...], axis=0, keepdims=True) * rate

    @pl.when(c == 0)
    def _():
        epad[0:8, :] = jnp.zeros((8, CH), F32)
        epad[8:16, :] = head[...]
        x = halo_ref[:, :CH] * keep_ref[0, 0]
        total = jnp.zeros((8, CH), F32)
        for j in range(CONVK):
            k = CONVK - 1 - j
            moved = epad[j : j + 8, :]
            sums_ref[k : k + 1, :] += jnp.sum(moved * x, axis=0, keepdims=True)
            total = total + cw_ref[k : k + 1, :] * moved
        edge_ref[...] = total * keep_ref[0, 0]


def spec(block, index):
    return pl.BlockSpec(block, index)


def whole(shape):
    return pl.BlockSpec(shape, lambda *_: (0,) * len(shape))


def scalar():
    return pl.BlockSpec(memory_space=pltpu.SMEM)


def shaped(shape, kind):
    return jax.ShapeDtypeStruct(shape, kind)


def cost(flops, moved):
    return pl.CostEstimate(flops=int(flops), bytes_accessed=int(moved), transcendentals=0)


def params(number=None):
    return pltpu.CompilerParams(
        dimension_semantics=("arbitrary",), vmem_limit_bytes=60 * 1024 * 1024, collective_id=number,
        has_side_effects=number is not None,
    )


LINE = 4


def my_place():
    f = lax.axis_index("fsdp")
    t = lax.axis_index("ctx")
    return f // 2, f % 2, t // 2, t % 2


def device_at(z, y, x, core):
    return {"fsdp": z * 2 + y, "ctx": x * 2 + core}


def order_of(z, y, x, core):
    return (z * 2 + y) * 4 + x * 2 + core


def box_peers():
    z, y, x, core = my_place()
    return [
        (None, device_at(z, y, x, 1 - core)), (None, device_at(z, y, 1 - x, core)),
        (None, device_at(z, 1 - y, x, core)),
        (z > 0, device_at(z - 1, y, x, core)), (z < LINE - 1, device_at(z + 1, y, x, core)),
    ]


def meet(peers):
    barrier = pltpu.get_barrier_semaphore()
    count = 0
    for valid, peer in peers:

        def greet(peer=peer):
            pl.semaphore_signal(barrier, inc=1, device_id=peer, device_id_type=pl.DeviceIdType.MESH)

        if valid is None:
            greet()
            count = count + 1
        else:
            pl.when(valid)(greet)
            count = count + jnp.where(valid, 1, 0)
    pl.semaphore_wait(barrier, count)


def send(src, dst, send_sem, recv_sem, peer):
    return pltpu.make_async_remote_copy(
        src_ref=src, dst_ref=dst, send_sem=send_sem, recv_sem=recv_sem,
        device_id=device_at(*peer), device_id_type=pl.DeviceIdType.MESH,
    )


class Gather:
    def __init__(self, own, out, recv, halves, twin, sent, here):
        self.own, self.out, self.rows = own, out, own.shape[0]
        self.recv, self.halves, self.twin, self.sent, self.here = recv, halves, twin, sent, here
        self.place = my_place()

    def block(self, z, y, x, core, half=None):
        size = self.rows if half is None else self.rows // 2
        start = order_of(z, y, x, core) * self.rows + (0 if half is None else half * size)
        return self.out.at[pl.ds(pl.multiple_of(start, 16), size)]

    def copy(self, origin, way, half=None, own=False):
        z, y, x, core = self.place
        oz, oy, ox = origin
        o = oz * 4 + oy * 2 + ox
        dst = self.block(oz, oy, ox, core, half)
        src = self.own if own else dst
        peer = {
            "up": (z + 1, y, x, core), "down": (z - 1, y, x, core), "x": (z, y, 1 - x, core),
            "y": (z, 1 - y, x, core), "twin": (z, y, x, 1 - core),
        }[way]
        sem = self.sent.at[("up", "down", "x", "y", "twin").index(way), o]
        if way == "twin":
            arrival = self.twin.at[o]
        elif half is not None:
            arrival = self.halves.at[half, o]
        else:
            arrival = self.recv.at[o]
        return send(src, dst, sem, arrival, peer)

    def arrived(self, origin, half=None):
        self.copy(origin, "x", half).wait_recv()

    def column(self, r):
        z = self.place[0]
        if r == 0:
            return [(None, z, True, True)]
        return [(z - r >= 0, z - r, True, False), (z + r < LINE, z + r, False, True)]

    def each(self, r, act):
        for valid, oz, below, above in self.column(r):
            if valid is None:
                act(oz, below, above)
            else:
                pl.when(valid)(lambda oz=oz, below=below, above=above: act(oz, below, above))

    def begin(self):
        z, y, x, core = self.place
        pltpu.make_async_copy(self.own, self.block(z, y, x, core), self.here).start()
        self.forward(0)

    def ways(self, oz, below, above, act):
        z = self.place[0]
        if below:
            pl.when(z < LINE - 1)(lambda: act("up"))
        if above:
            pl.when(z > 0)(lambda: act("down"))
        act("x")
        act("y")
        act("twin")

    def forward(self, r):
        z, y, x, core = self.place

        def act(oz, below, above):
            origin = (oz, y, x)
            if r:
                self.arrived(origin)
            self.ways(oz, below, above, lambda way: self.copy(origin, way, own=r == 0).start())

        self.each(r, act)

    def across(self, r):
        z, y, x, core = self.place

        def act(oz, below, above):
            self.arrived((oz, y, 1 - x))
            self.copy((oz, y, 1 - x), "y", 0).start()
            self.copy((oz, y, 1 - x), "twin").start()
            self.arrived((oz, 1 - y, x))
            self.copy((oz, 1 - y, x), "x", 1).start()
            self.copy((oz, 1 - y, x), "twin").start()

        self.each(r, act)

    def corner(self, r):
        z, y, x, core = self.place

        def act(oz, below, above):
            origin = (oz, 1 - y, 1 - x)
            self.arrived(origin, 0)
            self.arrived(origin, 1)
            self.copy(origin, "twin").start()

        self.each(r, act)

    def finish(self):
        z, y, x, core = self.place
        pltpu.make_async_copy(self.own, self.block(z, y, x, core), self.here).wait()
        for r in range(LINE):

            def act(oz, below, above, r=r):
                self.ways(oz, below, above, lambda way: self.copy((oz, y, x), way, own=r == 0).wait_send())
                self.copy((oz, y, 1 - x), "y", 0).wait_send()
                self.copy((oz, 1 - y, x), "x", 1).wait_send()
                for oy, ox in ((y, 1 - x), (1 - y, x), (1 - y, 1 - x)):
                    self.copy((oz, oy, ox), "twin").wait_send()
                for oy, ox in ((y, x), (y, 1 - x), (1 - y, x), (1 - y, 1 - x)):
                    self.copy((oz, oy, ox), "twin").wait_recv()

            self.each(r, act)

    def steps(self):
        return [
            self.begin,
            lambda: self.forward(1),
            lambda: self.across(0),
            lambda: self.forward(2),
            lambda: self.across(1),
            lambda: (self.forward(3), self.corner(0)),
            lambda: self.across(2),
            lambda: self.corner(1),
            lambda: self.across(3),
            lambda: (self.corner(2), self.corner(3)),
            self.finish,
        ]


def gather_scratch():
    dma = pltpu.SemaphoreType.DMA
    return [dma((16,)), dma((2, 16)), dma((16,)), dma((5, 16)), dma(())]


def gather_kernel(count, *refs):
    own, out, sems = refs[:count], refs[count : 2 * count], refs[2 * count :]
    meet(box_peers())
    lists = [
        Gather(own[k], out[k], *sems[5 * k : 5 * k + 5]).steps() for k in range(count)
    ]
    length = len(lists[0])
    for at in range(length + 2 * (count - 1)):
        for k in range(count):
            if 0 <= at - 2 * k < length:
                lists[k][at - 2 * k]()


def gathered(arrays, number):
    count = len(arrays)
    anywhere = pl.BlockSpec(memory_space=pl.ANY)
    return pl.pallas_call(
        lambda *refs: gather_kernel(count, *refs),
        in_specs=[anywhere] * count,
        out_specs=[anywhere] * count,
        out_shape=[shaped((32 * a.shape[0], a.shape[1]), a.dtype) for a in arrays],
        scratch_shapes=gather_scratch() * count,
        compiler_params=pltpu.CompilerParams(collective_id=number, has_side_effects=True),
        name="gather",
    )(*arrays)


class Scatter:
    def __init__(self, parts, out, got, kept, mixed_y, mixed_x, from_x, from_y, up, down, sems):
        self.parts, self.out = parts, out
        self.got, self.kept = got, kept
        self.mixed = (mixed_y, mixed_x)
        self.sides = (from_x, from_y)
        self.up, self.down = up, down
        self.twin_sent, self.twin_recv, self.sent, self.recv, self.line_sent, self.line_recv = sems
        self.place = my_place()
        self.rows = kept.shape[-2]
        self.last = kept.shape[0] - 1

    def groups(self):
        z, y, x, core = self.place
        return [(1 - y, 1 - x), (y, 1 - x), (1 - y, x), (y, x)]

    def to_twin(self, k):
        z, y, x, core = self.place
        gy, gx = self.groups()[k]
        return send(
            self.parts.at[:, gy * 4 + gx * 2 + 1 - core], self.got.at[k], self.twin_sent.at[k], self.twin_recv.at[k],
            (z, y, x, 1 - core),
        )

    def begin(self):
        for k in range(4):
            self.to_twin(k).start()

    def add(self, k, sources, first=0, rows=None):
        rows = self.rows if rows is None else rows
        pieces = rows // 16

        def piece(n, unused):
            b = n // pieces
            at = (n - b * pieces) * 16
            here = pl.ds(pl.multiple_of(first + at, 16), 16)
            total = None
            for source in sources:
                term = source(b, pl.multiple_of(at, 16), here).astype(F32)
                total = term if total is None else total + term
            self.kept[k, b, here] = total.astype(BF16)
            return unused

        lax.fori_loop(0, LINE * pieces, piece, 0)

    def own(self, k):
        return lambda b, at, here: self.kept[k, b, here]

    def both(self, k):
        z, y, x, core = self.place
        gy, gx = self.groups()[k]
        self.to_twin(k).wait_recv()
        self.add(
            k, [lambda b, at, here: self.parts[b, gy * 4 + gx * 2 + core, here], lambda b, at, here: self.got[k, b, here]]
        )

    def corner_copy(self, half):
        z, y, x, core = self.place
        size = self.rows // 2
        src = self.kept.at[0, :, pl.ds(half * size, size)]
        peer = (z, 1 - y, x, core) if half == 0 else (z, y, 1 - x, core)
        return send(src, self.mixed[half], self.sent.at[half], self.recv.at[half], peer)

    def side_copy(self, k):
        z, y, x, core = self.place
        peer = (z, y, 1 - x, core) if k == 1 else (z, 1 - y, x, core)
        return send(self.kept.at[k], self.sides[k - 1], self.sent.at[1 + k], self.recv.at[1 + k], peer)

    def corners(self):
        self.both(0)
        self.corner_copy(0).start()
        self.corner_copy(1).start()
        self.both(1)
        self.both(2)
        self.both(3)

    def sides_out(self):
        size = self.rows // 2
        for half, k in ((0, 1), (1, 2)):
            self.corner_copy(half).wait_recv()
            self.add(
                k, [self.own(k), lambda b, at, here, half=half: self.mixed[half][b, pl.ds(at, 16)]],
                half * size, size,
            )
            self.side_copy(k).start()

    def sides_in(self):
        self.side_copy(1).wait_recv()
        self.side_copy(2).wait_recv()
        self.add(
            3,
            [
                self.own(3), lambda b, at, here: self.sides[0][b, here], lambda b, at, here: self.sides[1][b, here],
            ],
        )

    def line_copy(self, oz, way):
        z, y, x, core = self.place
        buffer = self.up if way == 0 else self.down
        peer = (z + 1, y, x, core) if way == 0 else (z - 1, y, x, core)
        return send(
            self.kept.at[self.last, oz], buffer.at[oz], self.line_sent.at[way, oz], self.line_recv.at[way, oz], peer
        )

    def add_line(self, oz, buffer):
        def piece(n, unused):
            here = pl.ds(pl.multiple_of(n * 16, 16), 16)
            total = self.kept[self.last, oz, here].astype(F32) + buffer[oz, here].astype(F32)
            self.kept[self.last, oz, here] = total.astype(BF16)
            return unused

        lax.fori_loop(0, self.rows // 16, piece, 0)

    def line(self, r):
        z = self.place[0]

        def upward():
            oz = z + r

            @pl.when(z > 0)
            def _():
                self.line_copy(oz, 0).wait_recv()
                self.add_line(oz, self.up)

            self.line_copy(oz, 0).start()

        def downward():
            oz = z - r

            @pl.when(z < LINE - 1)
            def _():
                self.line_copy(oz, 1).wait_recv()
                self.add_line(oz, self.down)

            self.line_copy(oz, 1).start()

        pl.when(z + r < LINE)(upward)
        pl.when(z - r >= 0)(downward)

    def plane_sent(self):
        for k in range(4):
            self.to_twin(k).wait_send()
        for half in range(2):
            self.corner_copy(half).wait_send()
        for k in (1, 2):
            self.side_copy(k).wait_send()

    def hand_on(self, out):
        self.sides_in()
        out[...] = self.kept[self.last]
        self.plane_sent()

    def line_done(self):
        z = self.place[0]
        self.out[...] = self.kept[self.last, z].astype(F32)

        @pl.when(z > 0)
        def _():
            self.line_copy(z, 0).wait_recv()
            self.out[...] += self.up[z].astype(F32)

        @pl.when(z < LINE - 1)
        def _():
            self.line_copy(z, 1).wait_recv()
            self.out[...] += self.down[z].astype(F32)

        for r in range(1, LINE):
            pl.when(z + r < LINE)(lambda r=r: self.line_copy(z + r, 0).wait_send())
            pl.when(z - r >= 0)(lambda r=r: self.line_copy(z - r, 1).wait_send())

    def finish(self):
        self.line_done()
        self.plane_sent()

    def steps(self):
        return [
            self.begin, self.corners, self.sides_out, self.sides_in, lambda: self.line(3), lambda: self.line(2),
            lambda: self.line(1), self.finish,
        ]


def scatter_scratch(rows, columns):
    dma = pltpu.SemaphoreType.DMA
    half = rows // 2
    return [
        pltpu.VMEM((4, LINE, rows, columns), BF16),
        pltpu.VMEM((4, LINE, rows, columns), BF16),
        pltpu.VMEM((LINE, half, columns), BF16),
        pltpu.VMEM((LINE, half, columns), BF16),
        pltpu.VMEM((LINE, rows, columns), BF16),
        pltpu.VMEM((LINE, rows, columns), BF16),
        pltpu.VMEM((LINE, rows, columns), BF16),
        pltpu.VMEM((LINE, rows, columns), BF16),
        dma((4,)), dma((4,)), dma((4,)), dma((4,)), dma((2, LINE)), dma((2, LINE)),
    ]


class Total:
    def __init__(self, own, out, held, got, sent, recv):
        self.own, self.out, self.held, self.got, self.sent, self.recv = own, out, held, got, sent, recv

    def copy(self, k):
        z, y, x, core = my_place()
        near = z + 1 - 2 * (z % 2)
        peer = [
            (z, y, x, 1 - core), (z, y, 1 - x, core), (z, 1 - y, x, core), (near, y, x, core),
            ((z + 2) % LINE, y, x, core),
        ][k]
        return send(self.own if k == 0 else self.held.at[k], self.got.at[k], self.sent.at[k], self.recv.at[k], peer)

    def begin(self):
        self.copy(0).start()

    def turn(self, k):
        self.copy(k).wait_recv()
        mine = self.own[...] if k == 0 else self.held[k]
        total = mine + self.got[k]
        if k < 4:
            self.held[k + 1] = total
            self.copy(k + 1).start()
        else:
            self.out[...] = total

    def finish(self):
        for k in range(5):
            self.copy(k).wait_send()

    def steps(self):
        return [self.begin] + [lambda k=k: self.turn(k) for k in range(5)] + [self.finish]


WIDE = 256
SPLIT = 1280


def final_kernel(*refs):
    (
        turned_ref, du_cols, dz_ref, du_ref, tok_ref, cot_ref, gain_ref, wz_any, wu_any, gate_ref, conv_ref, gsum_ref,
        small_ref,
    ) = refs[:13]
    grad_ref, inw_ref, sums_ref = refs[13:16]
    (
        wz, wu, sems, parts_a, parts_b, out_a, out_b, packed, normed_grad, held, got, sent, recv,
    ) = refs[16:29]
    i = pl.program_id(0)
    steps = pl.num_programs(0) - tok_blocks(turned_ref)
    z, y, x, core = my_place()
    scr_a, scr_b = refs[29:43], refs[43:57]
    sum_a = Scatter(parts_a, out_a, *scr_a[:8], scr_a[8:])
    sum_b = Scatter(parts_b, out_b, *scr_b[:8], scr_b[8:])
    small = Total(packed, sums_ref, held, got, sent, recv)
    load_z = pltpu.make_async_copy(wz_any, wz, sems.at[0])
    load_u = pltpu.make_async_copy(wu_any, wu, sems.at[1])

    @pl.when(i == 0)
    def _():
        load_z.start()
        load_u.start()
        meet(box_peers() + [(None, device_at((z + 2) % LINE, y, x, core))])
        packed[...] = jnp.zeros_like(packed)
        packed[0:5, :] = conv_ref[0:5, :]
        packed[5:6, :DI] = gsum_ref[0:1, :]
        packed[5:6, DI : DI + 128] = small_ref[0:1, :]
        packed[5:6, DI + 128 :] = small_ref[1:2, :]
        packed[6:7, :DI] = gsum_ref[1:2, :]
        inw_ref[:, :DI] = gate_ref[...]

    plan = [
        (20, sum_a.begin), (32, sum_a.corners), (40, sum_b.begin), (42, sum_a.sides_out), (47, sum_b.corners),
        (52, sum_a.sides_in), (53, lambda: sum_a.line(3)), (54, sum_b.sides_out),
    ]

    @pl.when(i < steps)
    def _():
        when_at(4 * i, plan[:2])
        result = nn(turned_ref[...], du_cols[...]).astype(BF16)
        rows = parts_a.shape[2]

        def keep(parts, cols, width):
            for b in range(LINE):
                for q in range(8):
                    first = (b * 8 + q) * rows
                    parts[b, q, :, cols] = result[first : first + rows, :width]

        edge = SPLIT // WIDE

        @pl.when(i < edge)
        def _():
            keep(parts_a, pl.ds(pl.multiple_of(i * WIDE, WIDE), WIDE), WIDE)

        @pl.when(jnp.logical_and(i >= edge, i < steps - 1))
        def _():
            keep(parts_b, pl.ds(pl.multiple_of((i - edge) * WIDE, WIDE), WIDE), WIDE)

        @pl.when(i == steps - 1)
        def _():
            keep(parts_b, slice((steps - 1 - edge) * WIDE, UW - SPLIT), UW - SPLIT - (steps - 1 - edge) * WIDE)

    @pl.when(i == steps)
    def _():
        load_z.wait()
        load_u.wait()

    @pl.when(i >= steps)
    def _():
        width = tok_ref.shape[1]
        chunk = width // 4

        def part(n, unused):
            when_at(4 * i + n, plan[2:])
            feats = pl.ds(pl.multiple_of(n * chunk, chunk), chunk)
            normed_grad[:, feats] = nt(dz_ref[...], wz[feats, :]) + nt(du_ref[...], wu[feats, :])
            return unused

        lax.fori_loop(0, 4, part, 0)
        values = tok_ref[...].astype(F32)
        scale = lax.rsqrt(jnp.sum(values * values, axis=1, keepdims=True) * (1.0 / width) + epsilon)
        hat = values * scale
        grad = normed_grad[...]
        packed[7:8, :width] += jnp.sum(grad * hat, axis=0, keepdims=True)
        inner = grad * gain_ref[...]
        mean = jnp.sum(inner * hat, axis=1, keepdims=True) * (1.0 / width)
        grad_ref[...] = cot_ref[...].astype(F32) + scale * (inner - hat * mean)

    @pl.when(i == pl.num_programs(0) - 1)
    def _():
        small.begin()
        sum_a.line(2)
        small.turn(0)
        sum_a.line(1)
        small.turn(1)
        sum_b.sides_in()
        sum_b.line(3)
        sum_a.finish()
        small.turn(2)
        sum_b.line(2)
        small.turn(3)
        sum_b.line(1)
        small.turn(4)
        sum_b.finish()
        small.finish()
        inw_ref[:, DI : DI + SPLIT] = out_a[...]
        inw_ref[:, DI + SPLIT :] = out_b[:, : DPROJ - DI - SPLIT]


def tok_blocks(turned_ref):
    return turned_ref.shape[1] // Q


def final(turned, du, dz, tokens, cotangent, gain, w_z, w_u, gate_columns, conv_sums, gate_sums, small, number):
    width, rows = turned.shape
    steps = -(-UW // WIDE)
    blocks = rows // Q
    dma = pltpu.SemaphoreType.DMA
    own = width // 32
    anywhere = pl.BlockSpec(memory_space=pl.ANY)
    later = lambda i: (jnp.maximum(i - steps, 0), 0)
    sums = (8, CH)
    return pl.pallas_call(
        final_kernel,
        grid=(steps + blocks,),
        in_specs=[
            whole((width, rows)),
            spec((rows, WIDE), lambda i: (0, jnp.minimum(i, steps - 1))),
            spec((Q, DI), later),
            spec((Q, UW), later),
            spec((Q, width), later),
            spec((Q, width), later),
            whole((1, width)),
            anywhere,
            anywhere,
            whole((own, DI)),
            whole(sums),
            whole((8, DI)),
            whole((8, 128)),
        ],
        out_specs=[spec((Q, width), later), whole((own, DPROJ)), whole(sums)],
        out_shape=[shaped((rows, width), F32), shaped((own, DPROJ), F32), shaped(sums, F32)],
        scratch_shapes=[
            pltpu.VMEM((width, DI), BF16),
            pltpu.VMEM((width, UW), BF16),
            dma((2,)),
            pltpu.VMEM((LINE, 8, own, SPLIT), BF16),
            pltpu.VMEM((LINE, 8, own, UW - SPLIT), BF16),
            pltpu.VMEM((own, SPLIT), F32),
            pltpu.VMEM((own, UW - SPLIT), F32),
            pltpu.VMEM(sums, F32),
            pltpu.VMEM((Q, width), F32),
            pltpu.VMEM((5,) + sums, F32),
            pltpu.VMEM((5,) + sums, F32),
            dma((5,)),
            dma((5,)),
        ]
        + scatter_scratch(own, SPLIT)
        + scatter_scratch(own, UW - SPLIT),
        compiler_params=params(number),
        cost_estimate=cost(20e9, 60e6),
        name="final",
    )(turned, du, dz, du, tokens, cotangent, gain, w_z, w_u, gate_columns, conv_sums, gate_sums, small)


def local(
    tokens,
    valid_mask,
    stretch_start,
    cotangent,
    norm_gain,
    in_weight,
    conv_weight,
    conv_bias,
    step_bias,
    decay_log,
    skip_gain,
    gate_gain,
    out_weight,
):
    axes = ("fsdp", "ctx")
    rows, width = tokens.shape
    blocks = rows // Q
    near = lax.axis_size("ctx")
    halo_tokens = lax.ppermute(
        tokens[rows - 8 :], "ctx", [(k, k + 1) for k in range(near - 1)]
    )
    own_u = jnp.pad(in_weight[:, DI:], ((0, 0), (0, UW - (DPROJ - DI))))
    own_z = in_weight[:, :DI]
    boxed = lax.axis_size("fsdp") == 8 and near == 4
    if boxed:
        (w_u,) = gathered([own_u], 1)
        later = [own_z, out_weight]
    else:
        w_u, w_z, w_o = [lax.all_gather(a, axes, axis=0, tiled=True) for a in (own_u, own_z, out_weight)]
        later = []
    extra = len(later)
    anywhere = pl.BlockSpec(memory_space=pl.ANY)

    def hats(values):
        wide = values.astype(F32)
        return wide * lax.rsqrt(jnp.mean(wide * wide, axis=-1, keepdims=True) + epsilon)

    normed_more = (hats(jnp.concatenate([tokens, halo_tokens], 0)) * norm_gain).astype(BF16)
    normed = normed_more[:rows]
    valid = jnp.broadcast_to(valid_mask.astype(F32)[:, None], (rows, 128))
    keep = (1.0 - stretch_start[0].astype(F32)).reshape(1, 1)
    taps = conv_weight
    shift = conv_bias.reshape(1, CH)
    bias = jnp.pad(step_bias, (0, 128 - HEADS)).reshape(1, 128)
    logs = jnp.pad(decay_log, (0, 128 - HEADS)).reshape(1, 128)
    skips = jnp.repeat(skip_gain, P_SIZE).reshape(1, DI)
    u = jnp.dot(normed_more, w_u, preferred_element_type=F32)
    halo_block = rows // 8

    same = lambda c: (c, 0)
    same3 = lambda c: (c, 0, 0)
    one = lambda i: (jnp.minimum(i, blocks - 1), 0)
    one3 = lambda i: (jnp.minimum(i, blocks - 1), 0, 0)
    two = lambda i: (jnp.maximum(i - blocks, 0), 0)
    val, vp, conv, bc, ssd, ent, logd, step, cum, start, *filled = pl.pallas_call(
        lambda *refs: forward_kernel(extra, *refs),
        grid=(2 * blocks,),
        in_specs=[
            spec((Q, UW), one),
            spec((8, UW), lambda c: (halo_block, 0)),
            spec((Q, 128), one),
            scalar(),
            whole((CONVK, CH)),
            whole((1, CH)),
            whole((1, 128)),
            whole((1, 128)),
            whole((1, DI)),
        ]
        + [anywhere] * extra,
        out_specs=[
            spec((Q, DI), one),
            spec((Q, DI), one),
            spec((Q, CH), one),
            spec((Q, 2 * N), one),
            spec((Q, DI), two),
            spec((1, N, DI), one3),
            spec((Q, 128), one),
            spec((Q, 128), one),
            whole((blocks + 1, 8, DI)),
            whole((N, DI)),
        ]
        + [anywhere] * extra,
        out_shape=[
            shaped((rows, DI), BF16),
            shaped((rows, DI), BF16),
            shaped((rows, CH), BF16),
            shaped((rows, 2 * N), BF16),
            shaped((rows, DI), BF16),
            shaped((blocks, N, DI), BF16),
            shaped((rows, 128), F32),
            shaped((rows, 128), F32),
            shaped((blocks + 1, 8, DI), F32),
            shaped((N, DI), BF16),
        ]
        + [shaped((32 * a.shape[0], a.shape[1]), a.dtype) for a in later],
        scratch_shapes=[
            pltpu.VMEM((8, CH), F32),
            pltpu.VMEM((GROUPS, Q, 128), F32),
            pltpu.VMEM((128, DI), BF16),
            pltpu.VMEM((GROUPS, 8, Q), F32),
            pltpu.VMEM((Q, Q), F32),
            pltpu.VMEM((N, DI), F32),
            pltpu.VMEM((blocks, Q, DI), BF16),
            pltpu.VMEM((blocks, Q, DI), BF16),
            pltpu.VMEM((blocks, Q, 2 * N), BF16),
            pltpu.VMEM((blocks, Q, 128), F32),
            pltpu.VMEM((N, DI), BF16),
            pltpu.VMEM((N, DI), BF16),
            pltpu.SemaphoreType.DMA((2,)),
        ]
        + gather_scratch() * extra,
        compiler_params=params(2),
        cost_estimate=cost(15e9, 60e6),
        name="forward",
    )(u, u, valid, keep, taps, shift, bias, logs, skips, *later)
    if later:
        w_z, w_o = filled

    z = jnp.dot(normed, w_z, preferred_element_type=F32).astype(BF16)
    back = lambda i: (blocks - 1 - i, 0)
    back3 = lambda i: (blocks - 1 - i, 0, 0)
    gains = gate_gain.reshape(1, DI)
    output, gated, branch_grad, ds, dz, entt, gnext, gout, dlp, dc, gate_sums = pl.pallas_call(
        gate_kernel,
        grid=(blocks,),
        in_specs=[
            whole((N, DI)),
            spec((Q, DI), back),
            spec((1, N, DI), back3),
            spec((Q, DI), back),
            spec((Q, DI), back),
            spec((Q, 2 * N), back),
            spec((Q, 128), back),
            whole((blocks + 1, 8, DI)),
            spec((Q, width), back),
            spec((Q, width), back),
            spec((Q, 128), back),
            whole((DI, width)),
            whole((1, DI)),
        ],
        out_specs=[
            spec((Q, width), back),
            spec((Q, DI), back),
            spec((Q, width), back),
            spec((Q, DI), back),
            spec((Q, DI), back),
            spec((1, N, DI), back3),
            spec((1, N, DI), back3),
            whole((N, DI)),
            spec((Q, 128), back),
            spec((Q, N), back),
            whole((8, DI)),
        ],
        out_shape=[
            shaped((rows, width), BF16),
            shaped((rows, DI), BF16),
            shaped((rows, width), BF16),
            shaped((rows, DI), BF16),
            shaped((rows, DI), BF16),
            shaped((blocks, N, DI), BF16),
            shaped((blocks, N, DI), BF16),
            shaped((N, DI), BF16),
            shaped((rows, 128), F32),
            shaped((rows, N), F32),
            shaped((8, DI), F32),
        ],
        scratch_shapes=[
            pltpu.VMEM((N, DI), F32),
            pltpu.VMEM((N, DI), F32),
            pltpu.VMEM((128, DI), BF16),
            pltpu.VMEM((Q, DI), F32),
            pltpu.VMEM((Q, DI), F32),
            pltpu.VMEM((Q, DI), F32),
            pltpu.VMEM((Q, DI), F32),
            pltpu.VMEM((Q, DI), F32),
            pltpu.VMEM((Q, 128), F32),
        ],
        compiler_params=params(),
        cost_estimate=cost(15e9, 60e6),
        name="gate",
    )(
        start, ssd, ent, z, val, bc, logd, cum, tokens, cotangent, valid, w_o, gains,
    )

    def columns_of(left, right):
        return lax.dot_general(
            left, right, (((0,), (0,)), ((), ())), preferred_element_type=F32
        ).astype(BF16)

    def in_blocks(a):
        return a.reshape(LINE, 8, a.shape[0] // 32, a.shape[1])

    out_weight_grad = columns_of(gated, branch_grad)
    gate_columns = columns_of(normed, dz)
    mixing_parts = [in_blocks(out_weight_grad)] if boxed else []

    dvp, dbc, dlt, gin, *summed_out = pl.pallas_call(
        lambda *refs: mixing_kernel(len(mixing_parts), *refs),
        grid=(blocks,),
        in_specs=[
            spec((Q, DI), same),
            spec((Q, DI), same),
            spec((Q, 2 * N), same),
            spec((Q, 128), same),
            scalar(),
            whole((N, DI)),
            whole((blocks + 1, 8, DI)),
        ]
        + [pl.BlockSpec(memory_space=pltpu.VMEM) for a in mixing_parts],
        out_specs=[spec((Q, DI), same), spec((Q, 2 * N), same), spec((Q, 128), same), whole((N, DI))]
        + [whole((LINE,) + a.shape[-2:]) for a in mixing_parts],
        out_shape=[
            shaped((rows, DI), BF16), shaped((rows, 2 * N), F32), shaped((rows, 128), F32), shaped((N, DI), BF16),
        ]
        + [shaped((LINE,) + a.shape[-2:], BF16) for a in mixing_parts],
        scratch_shapes=[
            pltpu.VMEM((GROUPS, Q, 128), F32),
            pltpu.VMEM((GROUPS, 8, Q), F32),
            pltpu.VMEM((Q, Q), F32),
            pltpu.VMEM((Q, Q), F32),
            pltpu.VMEM((GROUPS, 8, Q), F32),
            pltpu.VMEM((128, Q), F32),
            pltpu.VMEM((GROUPS, Q, 128), F32),
            pltpu.VMEM((N, DI), BF16),
            pltpu.VMEM((N, DI), BF16),
            pltpu.SemaphoreType.DMA((2,)),
        ]
        + [each for a in mixing_parts for each in plane_scratch(*a.shape[-2:])],
        compiler_params=params(3),
        cost_estimate=cost(15e9, 60e6),
        name="mixing",
    )(ds, vp, bc, logd, keep, gout, cum, *mixing_parts)

    back_parts = summed_out + [in_blocks(gate_columns)] if boxed else []
    du, last, edge, conv_sums, small, *summed_gate = pl.pallas_call(
        lambda *refs: back_kernel(len(back_parts), *refs),
        grid=(blocks,),
        in_specs=[
            scalar(),
            whole((N, DI)),
            spec((1, N, DI), back3),
            spec((1, N, DI), back3),
            whole((blocks + 1, 8, DI)),
            spec((Q, DI), back),
            spec((Q, DI), back),
            spec((Q, DI), back),
            spec((Q, DI), back),
            spec((Q, CH), back),
            spec((Q, UW), back),
            spec((8, UW), lambda i: (halo_block, 0)),
            spec((Q, 2 * N), back),
            spec((Q, 128), back),
            spec((Q, 128), back),
            spec((Q, 128), back),
            spec((Q, 128), back),
            spec((Q, 128), back),
            spec((Q, 2 * N), back),
            spec((Q, N), back),
            whole((CONVK, CH)),
            whole((1, 128)),
            whole((1, 128)),
            whole((1, DI)),
        ]
        + [pl.BlockSpec(memory_space=pltpu.VMEM) for a in back_parts],
        out_specs=[
            spec((Q, UW), back),
            whole((8, CH)),
            whole((8, CH)),
            whole((8, CH)),
            whole((8, 128)),
        ]
        + [whole(a.shape[-2:]) for a in back_parts],
        out_shape=[
            shaped((rows, UW), BF16),
            shaped((8, CH), F32),
            shaped((8, CH), F32),
            shaped((8, CH), F32),
            shaped((8, 128), F32),
        ]
        + [shaped(a.shape[-2:], F32) for a in back_parts],
        scratch_shapes=[
            pltpu.VMEM((N, DI), F32),
            pltpu.VMEM((128, DI), BF16),
            pltpu.VMEM((8, CH), F32),
            pltpu.VMEM((16, CH), F32),
            pltpu.VMEM((Q, 128), F32),
            pltpu.VMEM((Q, 128), F32),
            pltpu.VMEM((16, 128), F32),
        ]
        + (
            scatter_scratch(*back_parts[1].shape[-2:]) + line_scratch(*back_parts[0].shape[-2:])
            if back_parts
            else []
        ),
        compiler_params=params(4 if back_parts else None),
        cost_estimate=cost(15e9, 60e6),
        name="back",
    )(
        keep, gin, gnext, entt, cum, vp, val, dvp, ds, conv, u, u, bc, logd, step, valid,
        dlp, dlt, dbc, dc, taps, bias, logs, skips, *back_parts,
    )
    edge_back = lax.ppermute(edge, "ctx", [(k + 1, k) for k in range(near - 1)])
    du = lax.dynamic_update_slice(du, (last + edge_back).astype(BF16), (rows - 8, 0))
    if boxed:
        out_weight_grad, gate_columns = summed_gate
        input_grad, in_weight_grad, sums = final(
            normed.T, du, dz, tokens, cotangent, norm_gain.reshape(1, width), w_z, w_u, gate_columns, conv_sums,
            gate_sums, small, 5,
        )
        return (
            output,
            input_grad,
            in_weight_grad,
            out_weight_grad,
            sums[7, :width],
            sums[:CONVK],
            sums[CONVK],
            sums[5, DI : DI + HEADS],
            sums[5, DI + 128 : DI + 128 + HEADS],
            jnp.sum(sums[6, :DI].reshape(HEADS, P_SIZE), axis=1),
            sums[5, :DI],
        )
    conv_columns = columns_of(normed, du)
    across = (((1,), (1,)), ((), ()))
    normed_grad = lax.dot_general(dz, w_z, across, preferred_element_type=F32) + lax.dot_general(
        du, w_u, across, preferred_element_type=F32
    )
    inputs = tokens.astype(F32)
    scale = lax.rsqrt(jnp.mean(inputs * inputs, axis=-1, keepdims=True) + epsilon)
    hat = inputs * scale
    inner = normed_grad * norm_gain
    input_grad = cotangent.astype(F32) + scale * (
        inner - hat * jnp.mean(inner * hat, axis=-1, keepdims=True)
    )
    norm_grad = jnp.sum(normed_grad * hat, axis=0)
    packed = jnp.concatenate(
        [
            norm_grad,
            conv_sums[:5].reshape(-1),
            gate_sums[:2].reshape(-1),
            small[:2].reshape(-1),
        ]
    )
    conv_columns, gate_columns, out_weight_grad = [
        lax.psum_scatter(a.astype(F32), axes, scatter_dimension=0, tiled=True)
        for a in (conv_columns, gate_columns, out_weight_grad)
    ]
    summed = lax.psum(packed, axes)
    in_weight_grad = jnp.concatenate([gate_columns, conv_columns[:, : DPROJ - DI]], 1)
    at = width
    conv_weight_grad = summed[at : at + CONVK * CH].reshape(CONVK, CH)
    at += CONVK * CH
    conv_bias_grad = summed[at : at + CH]
    at += CH
    gate_gain_grad = summed[at : at + DI]
    at += DI
    skip_gain_grad = jnp.sum(summed[at : at + DI].reshape(HEADS, P_SIZE), axis=1)
    at += DI
    step_bias_grad = summed[at : at + HEADS]
    decay_log_grad = summed[at + 128 : at + 128 + HEADS]
    return (
        output,
        input_grad,
        in_weight_grad,
        out_weight_grad,
        summed[:width],
        conv_weight_grad,
        conv_bias_grad,
        step_bias_grad,
        decay_log_grad,
        skip_gain_grad,
        gate_gain_grad,
    )


def solution(mesh):
    split = P(("fsdp", "ctx"), None)
    line = P(("fsdp", "ctx"))
    return jax.shard_map(
        local,
        mesh=mesh,
        in_specs=(split, line, line, split, P(), split, P(), P(), P(), P(), P(), P(), split),
        out_specs=(split, split, split, split, P(), P(), P(), P(), P(), P(), P()),
        check_vma=False,
    )
```

profile of v0, /device:TPU:0, one launch (start us, length us, event | category | flops | bytes accessed | tf_op | source)
XLA Modules:
  0.0 359.0 jit_solution(1805180575472771464)
XLA Ops:
  0.7 0.8 slice.36
  1.6 2.4 collective-permute-start
  4.0 1.2 pad_bitcast_fusion
  5.2 2.9 copy.25
  8.2 0.7 slice.39.refs_9_
  8.8 0.7 pad.11.refs_0_
  9.5 33.0 %gather.1.refs_8_ = bf16[1024,2432]{1,0:T(8,128)(2,1)} custom-call(bf16[32,2432]{1,0:T(8,128)(2,1)} %pad.11.refs_0_), custom_call_target="tpu_custom_call" | custom-call | tf_op jit(solution)/shard_map/gather/pallas_call | solution.py:934
  42.7 0.7 reshape_reshape.3.refs_8_.refs_23_
  43.4 0.6 reshape.59.refs_5_
  45.2 0.6 copy-done.2
  45.8 8.2 %fusion.7.refs_0_.refs_1_.refs_10_.refs_11_ = f32[1032,2432]{1,0:T(8,128)} fusion(bf16[1032,1024]{0,1:T(8,128)(2,1)S(1)} %fusion.2, bf16[1024,2432]{1,0:T(8,128)(2,1)S(1)} %copy-done.2), kind=kOutput, calls=%fused_computation.22 | convolution fusion | flops 5140119552 | bytes 17133568 | tf_op jit(solution)/shard_map/dot_general | solution.py:1393
  54.1 1.0 broadcast_in_dim.6.refs_2_.valid_ref.refs_15_
  55.1 60.6 %forward.1 = (bf16[1024,2048]{1,0:T(8,128)(2,1)}, bf16[1024,2048]{1,0:T(8,128)(2,1)}, bf16[1024,2304]{1,0:T(8,128)(2,1)}, bf16[1024,256]{1,0:T(8,128)(2,1)}, bf1...) custom-call(f32[1032,2432]{1,0:T(8,128)} %fusion.7.refs_0_.refs_1_.r, ...), custom_call_target="tpu_custom_call" | custom-call | flops 15000000512 | bytes 60000000 | tf_op jit(solution)/shard_map/forward/pallas_call | solution.py:1401
  115.6 8.3 %convolution_convert_fusion.2.z_ref = bf16[1024,2048]{1,0:T(8,128)(2,1)} fusion(bf16[1024,2048]{1,0:T(8,128)(2,1)} %get-tuple-element.52.refs_7_, bf16[1032,1024]{0,1:T(8,128)(2,1)S(1)} %copy-done.1), kind=kOutput, calls=%fused_computation.7 | convolution fusion | flops 4297064448 | bytes 10485760 | tf_op jit(solution)/shard_map/dot_general | solution.py:1465
  123.9 53.9 %gate.1 = (bf16[1024,1024]{1,0:T(8,128)(2,1)}, bf16[1024,2048]{1,0:T(8,128)(2,1)}, bf16[1024,1024]{1,0:T(8,128)(2,1)}, bf16[1024,2048]{1,0:T(8,128)(2,1)}, bf16[...) custom-call(bf16[128,2048]{1,0:T(8,128)(2,1)} %get-tuple-element.49., ...), custom_call_target="tpu_custom_call" | custom-call | flops 15000000512 | bytes 60000000 | tf_op jit(solution)/shard_map/gate/pallas_call | solution.py:1469
  177.8 8.4 %convolution_convert_fusion = bf16[1024,2048]{1,0:T(8,128)(2,1)} fusion(bf16[1024,2048]{1,0:T(8,128)(2,1)} %get-tuple-element.75.refs_2_, bf16[1032,1024]{0,1:T(8,128)(2,1)S(1)} %copy-done.1), kind=kOutput, calls=%fused_computation.5 | convolution fusion | flops 4297064448 | bytes 10485760 | tf_op jit(solution)/shard_map/dot_general | solution.py:1532
  186.2 6.2 %convolution_convert_fusion.1 = bf16[2048,1024]{1,0:T(8,128)(2,1)} fusion(bf16[1024,2048]{1,0:T(8,128)(2,1)S(1)} %copy-done.12, bf16[1024,1024]{1,0:T(8,128)(2,1)S(1)} %copy-done.13), kind=kOutput, calls=%fused_computation.6 | convolution fusion | flops 4297064448 | bytes 10485760 | tf_op jit(solution)/shard_map/dot_general | solution.py:1532
  192.4 36.6 %mixing.1 = (bf16[1024,2048]{1,0:T(8,128)(2,1)}, f32[1024,256]{1,0:T(8,128)}, f32[1024,128]{1,0:T(8,128)}, bf16[128,2048]{1,0:T(8,128)(2,1)}, bf16[4,64,1024]{2,1,0:T(8,128)(2,1)}) custom-call(bf16[1024,2048]{1,0:T(8,128)(2,1)} %get-tuple-element.59.refs_0_.refs_8_, bf16[1024,2048]{1,0:T(8,128)(2,1)} %get-tuple-element.60.refs_1_.refs_5_, ...), custom_call_target="tpu_custom_call" | custom-call | flops 15000000512 | bytes 60000000 | tf_op jit(solution)/shard_map/mixing/pallas_call | solution.py:1543
  229.0 55.0 %back.1 = (bf16[1024,2432]{1,0:T(8,128)(2,1)}, f32[8,2304]{1,0:T(8,128)}, f32[8,2304]{1,0:T(8,128)}, f32[8,2304]{1,0:T(8,128)}, f32[8,128]{1,0:T(8,128)}, /*index=5*/f32[64,1024]{1,0:T(8,128)}, f32[32,2048]{1,0:T(8,128)}) custom-call(f32[1,1]{1,0:T(1,128)} %bitcast.refs_3_.refs_4_.refs_0_, bf16[128,2048]{1,0:T(8,128)(2,1)} %get-tuple-element.64.refs_1_, ...), custom_call_target="tpu_custom_call" | custom-call | flops 15000000512 | bytes 60000000 | tf_op jit(solution)/shard_map/back/pallas_call | solution.py:1581
  284.0 1.7 collective-permute-start.1
  285.7 1.6 slice_bitcast_fusion.refs_0_
  287.5 0.6 fusion.5.refs_1_.refs_3_
  288.1 56.7 %final.1 = (f32[1024,1024]{1,0:T(8,128)}, f32[32,4384]{1,0:T(8,128)}, f32[8,2304]{1,0:T(8,128)}) custom-call(bf16[1024,1024]{1,0:T(8,128)(2,1)} %slice_bitcast_fusion.refs_0_, bf16[1024,2432]{1,0:T(8,128)(2,1)} %fusion.5.refs_1_.refs_3_, bf16[1024,2048]{1,0:T(8,128)(2,1)} %get-tuple-element.75.refs_2_, bf16[1024,2432]{1,0:T(8,128)(2,1)} %fusion.5.refs_1_.refs_3_, ...), custom_call_target="tpu_custom_call" | custom-call | flops 20000000000 | bytes 60000000 | tf_op jit(solution)/shard_map/final/pallas_call | solution.py:1303
  344.8 1.5 slice.42
  346.3 1.5 fusion.6
  347.8 1.5 slice_reduce_fusion
  349.4 1.4 slice.41
  350.7 1.2 slice_bitcast_fusion.1
  352.0 0.6 reduce_sum.19
  352.6 4.9 %copy.30 = f32[1024,1024]{1,0:T(8,128)} copy(f32[1024,1024]{1,0:T(8,128)} %get-tuple-element.105) | data formatting | bytes 8388608
  357.5 0.8 copy.31
  358.3 0.7 copy.32
  (38 shorter events, 1.7 us)
Async XLA Ops:
  0.6 7.5 %copy-start.3 = (bf16[32,4384]{1,0:T(8,128)(2,1)S(1)}, bf16[32,4384]{1,0:T(8,128)(2,1)}, u32[]{:S(2)}) copy-start(bf16[32,4384]{1,0:T(8,128)(2,1)} %param.18) | copy-start | bytes 841732
  0.7 8.2 %slice-start = ((bf16[32,4384]{1,0:T(8,128)(2,1)}), bf16[32,2336]{1,0:T(8,128)(2,1)S(1)}, s32[]{:S(2)}) async-start(bf16[32,4384]{1,0:T(8,128)(2,1)} %param.18), calls=%async_computation | async-start | bytes 311296 | tf_op jit(solution)/shard_map/slice | solution.py:1368
  1.6 42.4 %collective-permute-start = (bf16[8,1024]{0,1:T(8,128)(2,1)S(1)}, bf16[8,1024]{0,1:T(8,128)(2,1)S(1)}, u32[]{:S(2)}, u32[]{:S(2)}) collective-permute-start(bf16[8,1024]{0,1:T(8,128)(2,1)S(1)} %copy.24), channel_id=1, source_target_pairs={{0,1},{1,2},{2,3},{4,5},{5,6},{6,7},{8,9},{9,10},{10,11},{12,13},{... | collective-permute-start | bytes 49160 | tf_op jit(solution)/shard_map/ppermute | solution.py:1365
  5.2 37.3 %copy-start.8 = (s32[1024]{0:T(1024)S(1)}, s32[1024]{0:T(1024)}, u32[]{:S(2)}) copy-start(s32[1024]{0:T(1024)} %param.14) | copy-start | bytes 12292
  5.2 37.4 %copy-start.11 = (s32[4]{0:T(128)S(1)}, s32[4]{0:T(128)}, u32[]{:S(2)}) copy-start(s32[4]{0:T(128)} %param.15) | copy-start | bytes 52
  5.2 37.4 %copy-start.10 = (f32[32]{0:T(128)S(1)}, f32[32]{0:T(128)}, u32[]{:S(2)}) copy-start(f32[32]{0:T(128)} %param.23) | copy-start | bytes 388
  5.2 38.2 %copy-start.7 = (f32[2304]{0:T(1024)S(1)}, f32[2304]{0:T(1024)}, u32[]{:S(2)}) copy-start(f32[2304]{0:T(1024)} %param.20) | copy-start | bytes 27652
  8.1 36.4 %copy-start.9 = (f32[1024]{0:T(1024)S(1)}, f32[1024]{0:T(1024)}, u32[]{:S(2)}) copy-start(f32[1024]{0:T(1024)} %param.17) | copy-start | bytes 12292
  43.4 2.4 copy-start.2
  45.8 8.2 %copy-start = (bf16[1032,1024]{0,1:T(8,128)(2,1)}, bf16[1032,1024]{0,1:T(8,128)(2,1)S(1)}, u32[]{:S(2)}) copy-start(bf16[1032,1024]{0,1:T(8,128)(2,1)S(1)} %fusion.2) | copy-start | bytes 6340612
  55.1 60.6 %copy-start.1 = (bf16[1032,1024]{0,1:T(8,128)(2,1)S(1)}, bf16[1032,1024]{0,1:T(8,128)(2,1)}, u32[]{:S(2)}) copy-start(bf16[1032,1024]{0,1:T(8,128)(2,1)} %copy-done) | copy-start | bytes 6340612
  177.8 8.4 %copy-start.12 = (bf16[1024,2048]{1,0:T(8,128)(2,1)S(1)}, bf16[1024,2048]{1,0:T(8,128)(2,1)}, u32[]{:S(2)}) copy-start(bf16[1024,2048]{1,0:T(8,128)(2,1)} %get-tuple-element.62) | copy-start | bytes 12582916
  177.8 8.4 %copy-start.13 = (bf16[1024,1024]{1,0:T(8,128)(2,1)S(1)}, bf16[1024,1024]{1,0:T(8,128)(2,1)}, u32[]{:S(2)}) copy-start(bf16[1024,1024]{1,0:T(8,128)(2,1)} %get-tuple-element.63) | copy-start | bytes 6291460
  284.0 3.5 copy-start.6
  284.0 3.5 collective-permute-start.1
  352.6 4.9 %copy-start.4 = (f32[32,4384]{1,0:T(8,128)S(1)}, f32[32,4384]{1,0:T(8,128)}, u32[]{:S(2)}) copy-start(f32[32,4384]{1,0:T(8,128)} %get-tuple-element.106) | copy-start | bytes 1683460
  352.6 5.7 %copy-start.5 = (f32[64,1024]{1,0:T(8,128)S(1)}, f32[64,1024]{1,0:T(8,128)}, u32[]{:S(2)}) copy-start(f32[64,1024]{1,0:T(8,128)} %get-tuple-element.107) | copy-start | bytes 786436
where the time goes:
time: 360 us; the launch traced here: 359 us
  Pallas kernels  296 us (82%)
  matrix products  31.1 us (9%)
  local copies, waits for them, and re-layouts  24.6 us (7%)
  starting transfers between devices  4.1 us (1%)
    pallas_call x1, Pallas kernels, local(): pl.pallas_call(lambda *refs: forward_kernel(extra, *refs), grid=(2 * bloc...  60.6 us
    pallas_call x1, Pallas kernels, final(): pl.pallas_call(final_kernel, grid=(steps + blocks,), in_specs=[whole((wid...  56.7 us
    pallas_call x1, Pallas kernels, local(): pl.pallas_call(lambda *refs: back_kernel(len(back_parts), *refs), grid=(b...  55 us
    pallas_call x1, Pallas kernels, local(): pl.pallas_call(gate_kernel, grid=(blocks,), in_specs=[whole((N, DI)), spe...  53.9 us
    pallas_call x1, Pallas kernels, local(): pl.pallas_call(lambda *refs: mixing_kernel(len(mixing_parts), *refs), gri...  36.6 us
    pallas_call x1, Pallas kernels, gathered(): pl.pallas_call(lambda *refs: gather_kernel(count, *refs), in_specs=[anywh...  33 us
    dot_general x2, matrix products, columns_of(): lax.dot_general(left, right, (((0,), (0,)), ((), ())), preferred_element_...  14.6 us
    unnamed x32, local copies, waits for them, and re-layouts  9.96 us
  transfers between devices with their start and end apart: 2, of which 1 were waited for; matrix products, arithmetic and copies ran while one was open for 2% of the time, Pallas kernels for 9%

commit v1 on v0

--- a/solution.py
+++ b/solution.py
@@ -17,6 +17,7 @@
 GW = 256
 GROUPS = DI // GW
 HALF = Q // 2
+HALO = 16
 
 F32 = jnp.float32
 BF16 = jnp.bfloat16
@@ -149,17 +150,17 @@
 
 def forward_kernel(count, *refs):
     (
-        u_ref, halo_ref, valid_ref, keep_ref, cw_ref, cb_ref, sb_ref, dl_ref, skip_ref,
-    ) = refs[:9]
-    own = refs[9 : 9 + count]
+        normed_ref, halo_ref, wu_any, valid_ref, keep_ref, cw_ref, cb_ref, sb_ref, dl_ref, skip_ref,
+    ) = refs[:10]
+    own = refs[10 : 10 + count]
     (
-        val_ref, vp_ref, conv_ref, bc_ref, ssd_ref, ent_ref, log_ref, step_ref, cum_ref, start_ref,
-    ) = refs[9 + count : 19 + count]
-    outs = refs[19 + count : 19 + 2 * count]
+        val_ref, vp_ref, conv_ref, bc_ref, ssd_ref, ent_ref, log_ref, step_ref, cum_ref, start_ref, u_ref, ahead_ref,
+    ) = refs[10 + count : 22 + count]
+    outs = refs[22 + count : 22 + 2 * count]
     (
-        past, logs, picks, logt, inter, state, all_vp, all_val, all_bc, all_log, message, arrived, sems,
-    ) = refs[19 + 2 * count : 32 + 2 * count]
-    gather_sems = refs[32 + 2 * count :]
+        past, logs, picks, logt, inter, state, all_vp, all_val, all_bc, all_log, message, arrived, sems, wu, load, log_wide, step_wide,
+    ) = refs[22 + 2 * count : 39 + 2 * count]
+    gather_sems = refs[39 + 2 * count :]
     i = pl.program_id(0)
     blocks = pl.num_programs(0) // 2
     first = i < blocks
@@ -168,7 +169,7 @@
     pos = lax.axis_index("ctx")
     plan = []
     if count:
-        lists = [Gather(own[k], outs[k], *gather_sems[5 * k : 5 * k + 5]).steps() for k in range(count)]
+        lists = [Gather(own[k], outs[k], (0, outs[k].shape[1], 0), *gather_sems[5 * k : 5 * k + 5]).steps() for k in range(count)]
         length = len(lists[0])
         for at in range(length + 2 * (count - 1)):
             acts = [lists[k][at - 2 * k] for k in range(count) if 0 <= at - 2 * k < length]
@@ -176,9 +177,14 @@
 
     @pl.when(i == 0)
     def _():
+        fetch = pltpu.make_async_copy(wu_any, wu, load)
+        fetch.start()
+        fill_picks(picks)
         meet((box_peers() if count else []) + chain_peers())
-        past[...] = halo_ref[:, :CH] * keep_ref[0, 0]
-        fill_picks(picks)
+        fetch.wait()
+        before = nn(halo_ref[...], wu[...])[8:]
+        ahead_ref[...] = before
+        past[...] = before[:, :CH] * keep_ref[0, 0]
         state[...] = jnp.zeros_like(state)
         cum_ref[...] = jnp.zeros_like(cum_ref)
 
@@ -188,7 +194,9 @@
 
     @pl.when(first)
     def _():
-        raw = u_ref[:, CH:] + sb_ref[...]
+        tail = nn(normed_ref[...], wu[:, DI:])
+        u_ref[:, DI:] = tail
+        raw = tail[:, 2 * N :] + sb_ref[...]
         step = softplus(raw) * valid_ref[...]
         step = jnp.where(lanes_of(step.shape) < HEADS, step, 0.0)
         rate = -jnp.exp(dl_ref[...]) * LOG2E
@@ -199,8 +207,7 @@
         log_parts = in_parts(logd)
         step_parts = in_parts(step)
 
-        def convolved(cols):
-            x = u_ref[:, cols]
+        def convolved(cols, x):
             before = past[:, cols]
             past[:, cols] = x[Q - 8 :]
             total = cb_ref[:, cols] + cw_ref[CONVK - 1 : CONVK, cols] * x
@@ -208,8 +215,8 @@
                 total = total + cw_ref[k : k + 1, cols] * delayed(before, x, CONVK - 1 - k)
             return total
 
-        conv_b = convolved(pl.ds(DI, N))
-        conv_c = convolved(pl.ds(DI + N, N))
+        conv_b = convolved(pl.ds(DI, N), tail[:, :N])
+        conv_c = convolved(pl.ds(DI + N, N), tail[:, N : 2 * N])
         conv_ref[:, DI : DI + N] = conv_b.astype(BF16)
         conv_ref[:, DI + N :] = conv_c.astype(BF16)
         act_b = conv_b * sigmoid(conv_b)
@@ -220,21 +227,28 @@
         turned_b = act_b.T.astype(BF16)
         ent_ref[0] = state[...].astype(BF16)
 
+        def ahead(g):
+            cols = pl.ds(pl.multiple_of(g * GW, GW), GW)
+            slot = g % 2
+            u_ref[:, cols] = nn(normed_ref[...], wu[:, cols])
+            log_wide[slot] = nn(log_parts, picks[:, cols])
+            step_wide[slot] = nn(step_parts, picks[:, cols])
+
+        ahead(0)
+
         def group(g, unused):
             when_at(i * GROUPS + g, plan)
-            wide = pl.ds(pl.multiple_of(g * GW, GW), GW)
-            log_wide = nn(log_parts, picks[:, wide])
-            step_wide = nn(step_parts, picks[:, wide])
+            slot = g % 2
             for j in range(2):
                 cols = pl.ds(pl.multiple_of(g * GW + 128 * j, 128), 128)
-                cv = convolved(cols)
+                cv = convolved(cols, u_ref[:, cols])
                 conv_ref[:, cols] = cv.astype(BF16)
                 val = cv * sigmoid(cv)
                 low = val.astype(BF16)
                 val_ref[:, cols] = low
                 all_val[c, :, cols] = low
-                lp = log_wide[:, 128 * j : 128 * j + 128]
-                vp = val * step_wide[:, 128 * j : 128 * j + 128]
+                lp = log_wide[slot, :, 128 * j : 128 * j + 128]
+                vp = val * step_wide[slot, :, 128 * j : 128 * j + 128]
                 low = vp.astype(BF16)
                 vp_ref[:, cols] = low
                 all_vp[c, :, cols] = low
@@ -242,14 +256,14 @@
                 weighted = (vp * jnp.exp2(last - lp)).astype(BF16)
                 state[:, cols] = jnp.exp2(last) * state[:, cols] + nn(turned_b, weighted)
                 cum_ref[c + 1, :, cols] = cum_ref[c, :, cols] + last
+            ahead(lax.rem(g + 1, GROUPS))
             return unused
 
         lax.fori_loop(0, GROUPS, group, 0)
 
-    for k in range(near):
-
-        @pl.when(jnp.logical_and(i == blocks + k, pos == k))
-        def _(k=k):
+    def hop(k):
+        @pl.when(pos == k)
+        def _():
             if k:
                 pass_on(message, arrived, sems, 1).wait_recv()
                 entering = keep_ref[0, 0] * arrived[...].astype(F32)
@@ -263,6 +277,8 @@
                     message[...] = state[...].astype(BF16)
                 pass_on(message, arrived, sems, 1).start()
 
+    hops = [(blocks * GROUPS + FORWARD_HOPS[k], lambda k=k: hop(k)) for k in range(near)]
+
     @pl.when(jnp.logical_not(first))
     def _():
         logd = all_log[c]
@@ -274,6 +290,7 @@
 
         def group(g, unused):
             when_at(i * GROUPS + g, plan)
+            when_at(i * GROUPS + g, hops)
             lg = logs[g]
             for j in range(2):
                 cols = pl.ds(pl.multiple_of(g * GW + 128 * j, 128), 128)
@@ -417,6 +434,8 @@
 
 
 FORWARD_PLACES = tuple(5 * k for k in range(13))
+FORWARD_HOPS = (0, 8, 20, 30)
+MIXING_HOPS = (0, 8, 20, 30)
 MIXING_PLACES = (0, 5, 12, 31)
 LINE_PLACES = (1, 4, 8, 12)
 BACK_PLACES = (0, 4, 9, 19, 22, 25, 28, 31)
@@ -464,10 +483,9 @@
     def _():
         meet((box_peers() if count else []) + chain_peers())
 
-    for k in range(near):
-
-        @pl.when(jnp.logical_and(i == k, pos == near - 1 - k))
-        def _(k=k):
+    def hop(k):
+        @pl.when(pos == near - 1 - k)
+        def _():
             total = gout_ref[...].astype(F32)
             if k:
                 pass_on(message, arrived, sems, -1).wait_recv()
@@ -479,9 +497,7 @@
                 message[...] = (keep_ref[0, 0] * total).astype(BF16)
                 pass_on(message, arrived, sems, -1).start()
 
-    @pl.when(jnp.logical_and(i == blocks - 1, pos > 0))
-    def _():
-        pass_on(message, arrived, sems, -1).wait_send()
+    hops = [(MIXING_HOPS[k], lambda k=k: hop(k)) for k in range(near)]
 
     logd = log_ref[...]
     spread(logd, logs)
@@ -497,6 +513,7 @@
 
     def group(g, unused):
         when_at(i * GROUPS + g, plan)
+        when_at(i * GROUPS + g, hops)
         lg = logs[g]
         first_col = jnp.zeros((HALF, 128), F32)
         second_col = jnp.zeros((HALF, 128), F32)
@@ -570,6 +587,10 @@
     dbc_ref[:, :N] = nn(masked.astype(BF16), low_c)
     dbc_ref[:, N:] = nn(masked.T.astype(BF16), low_b)
 
+    @pl.when(jnp.logical_and(i == blocks - 1, pos > 0))
+    def _():
+        pass_on(message, arrived, sems, -1).wait_send()
+
 
 def back_kernel(count, *refs):
     (
@@ -783,15 +804,16 @@
 
 
 class Gather:
-    def __init__(self, own, out, recv, halves, twin, sent, here):
-        self.own, self.out, self.rows = own, out, own.shape[0]
+    def __init__(self, own, out, window, recv, halves, twin, sent, here):
+        first, self.width, self.at = window
+        self.own, self.out, self.rows = own.at[:, pl.ds(first, self.width)], out, own.shape[0]
         self.recv, self.halves, self.twin, self.sent, self.here = recv, halves, twin, sent, here
         self.place = my_place()
 
     def block(self, z, y, x, core, half=None):
         size = self.rows if half is None else self.rows // 2
         start = order_of(z, y, x, core) * self.rows + (0 if half is None else half * size)
-        return self.out.at[pl.ds(pl.multiple_of(start, 16), size)]
+        return self.out.at[pl.ds(pl.multiple_of(start, 16), size), pl.ds(self.at, self.width)]
 
     def copy(self, origin, way, half=None, own=False):
         z, y, x, core = self.place
@@ -915,31 +937,80 @@
     return [dma((16,)), dma((2, 16)), dma((16,)), dma((5, 16)), dma(())]
 
 
-def gather_kernel(count, *refs):
-    own, out, sems = refs[:count], refs[count : 2 * count], refs[2 * count :]
-    meet(box_peers())
-    lists = [
-        Gather(own[k], out[k], *sems[5 * k : 5 * k + 5]).steps() for k in range(count)
-    ]
-    length = len(lists[0])
-    for at in range(length + 2 * (count - 1)):
-        for k in range(count):
-            if 0 <= at - 2 * k < length:
-                lists[k][at - 2 * k]()
-
-
-def gathered(arrays, number):
-    count = len(arrays)
+U_WINDOWS = ((DI, 1280, 0), (DI + 1280, UW - 1280, 1280))
+
+
+def gather_kernel(own, tok_ref, gain_ref, out, normed_ref, turned_ref, near_rows, sems, *gather_sems):
+    rows, width = tok_ref.shape
+    meet(box_peers() + chain_peers())
+    pos = lax.axis_index("ctx")
+    last = pos == lax.axis_size("ctx") - 1
+    lists = [Gather(own, out, window, *gather_sems[5 * k : 5 * k + 5]).steps() for k, window in enumerate(U_WINDOWS)]
+    for each in lists:
+        each[0]()
+    halo = pass_on(tok_ref.at[pl.ds(rows - HALO, HALO)], near_rows, sems, 1)
+
+    @pl.when(jnp.logical_not(last))
+    def _():
+        halo.start()
+
+    def normed(values):
+        wide = values.astype(F32)
+        scale = lax.rsqrt(jnp.sum(wide * wide, axis=1, keepdims=True) * (1.0 / width) + epsilon)
+        return wide * scale * gain_ref[...]
+
+    def block(r, unused):
+        here = pl.ds(pl.multiple_of(r * 128, 128), 128)
+        values = normed(tok_ref[here, :])
+        normed_ref[here, :] = values.astype(BF16)
+        turned_ref[:, here] = values.T.astype(BF16)
+        return unused
+
+    def hops(at):
+        for k, each in enumerate(lists):
+            if 1 <= at - k < len(each):
+                each[at - k]()
+
+    parts = 4
+    for at in range(parts):
+        lax.fori_loop(at * rows // 128 // parts, (at + 1) * rows // 128 // parts, block, 0)
+        hops(at + 1)
+
+    @pl.when(pos > 0)
+    def _():
+        halo.wait_recv()
+
+    @pl.when(pos == 0)
+    def _():
+        near_rows[...] = jnp.zeros_like(near_rows)
+
+    normed_ref[rows:, :] = normed(near_rows[...]).astype(BF16)
+
+    @pl.when(jnp.logical_not(last))
+    def _():
+        halo.wait_send()
+
+    for at in range(parts + 1, len(lists[0]) + 1):
+        hops(at)
+
+
+def gathered(own, tokens, gain, number):
+    rows, width = tokens.shape
     anywhere = pl.BlockSpec(memory_space=pl.ANY)
+    vmem = pl.BlockSpec(memory_space=pltpu.VMEM)
     return pl.pallas_call(
-        lambda *refs: gather_kernel(count, *refs),
-        in_specs=[anywhere] * count,
-        out_specs=[anywhere] * count,
-        out_shape=[shaped((32 * a.shape[0], a.shape[1]), a.dtype) for a in arrays],
-        scratch_shapes=gather_scratch() * count,
-        compiler_params=pltpu.CompilerParams(collective_id=number, has_side_effects=True),
+        gather_kernel,
+        in_specs=[anywhere, vmem, vmem],
+        out_specs=[anywhere, vmem, vmem],
+        out_shape=[
+            shaped((32 * own.shape[0], UW), BF16), shaped((rows + HALO, width), BF16), shaped((width, rows), BF16),
+        ],
+        scratch_shapes=[pltpu.VMEM((HALO, width), BF16), pltpu.SemaphoreType.DMA((2,))] + gather_scratch() * 2,
+        compiler_params=pltpu.CompilerParams(
+            collective_id=number, has_side_effects=True, vmem_limit_bytes=60 * 1024 * 1024
+        ),
         name="gather",
-    )(*arrays)
+    )(own, tokens, gain)
 
 
 class Scatter:
@@ -1179,20 +1250,22 @@
 
 def final_kernel(*refs):
     (
-        turned_ref, du_cols, dz_ref, du_ref, tok_ref, cot_ref, gain_ref, wz_any, wu_any, gate_ref, conv_ref, gsum_ref,
+        turned_ref, du_cols, dz_ref, du_ref, tok_ref, gain_ref, wz_any, wu_any, gate_ref, conv_ref, gsum_ref,
         small_ref,
-    ) = refs[:13]
-    grad_ref, inw_ref, sums_ref = refs[13:16]
+    ) = refs[:12]
+    grad_ref, inw_ref, sums_ref, norm_ref = refs[12:16]
     (
-        wz, wu, sems, parts_a, parts_b, out_a, out_b, packed, normed_grad, held, got, sent, recv,
-    ) = refs[16:29]
+        wz, wu, sems, parts_a, parts_b, out_a, out_b, packed, normed_grad, held, got, sent, recv, gains,
+        gains_held, gains_got, gains_sent, gains_recv,
+    ) = refs[16:34]
     i = pl.program_id(0)
     steps = pl.num_programs(0) - tok_blocks(turned_ref)
     z, y, x, core = my_place()
-    scr_a, scr_b = refs[29:43], refs[43:57]
+    scr_a, scr_b = refs[34:48], refs[48:62]
     sum_a = Scatter(parts_a, out_a, *scr_a[:8], scr_a[8:])
     sum_b = Scatter(parts_b, out_b, *scr_b[:8], scr_b[8:])
     small = Total(packed, sums_ref, held, got, sent, recv)
+    norm = Total(gains, norm_ref, gains_held, gains_got, gains_sent, gains_recv)
     load_z = pltpu.make_async_copy(wz_any, wz, sems.at[0])
     load_u = pltpu.make_async_copy(wu_any, wu, sems.at[1])
 
@@ -1207,16 +1280,23 @@
         packed[5:6, DI : DI + 128] = small_ref[0:1, :]
         packed[5:6, DI + 128 :] = small_ref[1:2, :]
         packed[6:7, :DI] = gsum_ref[1:2, :]
+        gains[...] = jnp.zeros_like(gains)
+        small.begin()
         inw_ref[:, :DI] = gate_ref[...]
 
-    plan = [
-        (20, sum_a.begin), (32, sum_a.corners), (40, sum_b.begin), (42, sum_a.sides_out), (47, sum_b.corners),
-        (52, sum_a.sides_in), (53, lambda: sum_a.line(3)), (54, sum_b.sides_out),
+    first = [
+        (8, lambda: small.turn(0)), (20, lambda: (sum_a.begin(), small.turn(1))), (28, sum_a.corners),
+        (36, lambda: (sum_a.sides_out(), small.turn(2))),
     ]
+    second = [
+        (40, sum_b.begin), (43, sum_b.corners), (45, lambda: small.turn(3)),
+        (47, lambda: (sum_a.sides_in(), sum_a.line(3))), (49, sum_b.sides_out), (51, lambda: sum_a.line(2)),
+        (53, lambda: small.turn(4)), (55, lambda: sum_a.line(1)),
+    ]
 
     @pl.when(i < steps)
     def _():
-        when_at(4 * i, plan[:2])
+        when_at(4 * i, first)
         result = nn(turned_ref[...], du_cols[...]).astype(BF16)
         rows = parts_a.shape[2]
 
@@ -1251,7 +1331,7 @@
         chunk = width // 4
 
         def part(n, unused):
-            when_at(4 * i + n, plan[2:])
+            when_at(4 * i + n, second)
             feats = pl.ds(pl.multiple_of(n * chunk, chunk), chunk)
             normed_grad[:, feats] = nt(dz_ref[...], wz[feats, :]) + nt(du_ref[...], wu[feats, :])
             return unused
@@ -1261,28 +1341,27 @@
         scale = lax.rsqrt(jnp.sum(values * values, axis=1, keepdims=True) * (1.0 / width) + epsilon)
         hat = values * scale
         grad = normed_grad[...]
-        packed[7:8, :width] += jnp.sum(grad * hat, axis=0, keepdims=True)
+        gains[...] += jnp.sum(grad * hat, axis=0, keepdims=True)
         inner = grad * gain_ref[...]
         mean = jnp.sum(inner * hat, axis=1, keepdims=True) * (1.0 / width)
-        grad_ref[...] = cot_ref[...].astype(F32) + scale * (inner - hat * mean)
+        grad_ref[...] = (scale * (inner - hat * mean)).astype(BF16)
 
     @pl.when(i == pl.num_programs(0) - 1)
     def _():
-        small.begin()
-        sum_a.line(2)
-        small.turn(0)
-        sum_a.line(1)
-        small.turn(1)
+        norm.begin()
         sum_b.sides_in()
         sum_b.line(3)
+        norm.turn(0)
+        norm.turn(1)
+        sum_b.line(2)
+        norm.turn(2)
         sum_a.finish()
-        small.turn(2)
-        sum_b.line(2)
-        small.turn(3)
         sum_b.line(1)
-        small.turn(4)
+        norm.turn(3)
+        norm.turn(4)
         sum_b.finish()
         small.finish()
+        norm.finish()
         inw_ref[:, DI : DI + SPLIT] = out_a[...]
         inw_ref[:, DI + SPLIT :] = out_b[:, : DPROJ - DI - SPLIT]
 
@@ -1291,7 +1370,7 @@
     return turned_ref.shape[1] // Q
 
 
-def final(turned, du, dz, tokens, cotangent, gain, w_z, w_u, gate_columns, conv_sums, gate_sums, small, number):
+def final(turned, du, dz, tokens, gain, w_z, w_u, gate_columns, conv_sums, gate_sums, small, number):
     width, rows = turned.shape
     steps = -(-UW // WIDE)
     blocks = rows // Q
@@ -1309,7 +1388,6 @@
             spec((Q, DI), later),
             spec((Q, UW), later),
             spec((Q, width), later),
-            spec((Q, width), later),
             whole((1, width)),
             anywhere,
             anywhere,
@@ -1318,8 +1396,10 @@
             whole((8, DI)),
             whole((8, 128)),
         ],
-        out_specs=[spec((Q, width), later), whole((own, DPROJ)), whole(sums)],
-        out_shape=[shaped((rows, width), F32), shaped((own, DPROJ), F32), shaped(sums, F32)],
+        out_specs=[spec((Q, width), later), whole((own, DPROJ)), whole(sums), whole((1, width))],
+        out_shape=[
+            shaped((rows, width), BF16), shaped((own, DPROJ), F32), shaped(sums, F32), shaped((1, width), F32),
+        ],
         scratch_shapes=[
             pltpu.VMEM((width, DI), BF16),
             pltpu.VMEM((width, UW), BF16),
@@ -1334,13 +1414,67 @@
             pltpu.VMEM((5,) + sums, F32),
             dma((5,)),
             dma((5,)),
+            pltpu.VMEM((1, width), F32),
+            pltpu.VMEM((5, 1, width), F32),
+            pltpu.VMEM((5, 1, width), F32),
+            dma((5,)),
+            dma((5,)),
         ]
         + scatter_scratch(own, SPLIT)
         + scatter_scratch(own, UW - SPLIT),
         compiler_params=params(number),
         cost_estimate=cost(20e9, 60e6),
         name="final",
-    )(turned, du, dz, du, tokens, cotangent, gain, w_z, w_u, gate_columns, conv_sums, gate_sums, small)
+    )(turned, du, dz, du, tokens, gain, w_z, w_u, gate_columns, conv_sums, gate_sums, small)
+
+
+def close_kernel(
+    part_ref, cot_ref, inw_in, outw_in, sums_ref, norm_in, back_in,
+    grad_ref, inw_ref, outw_ref, norm_ref, taps_ref, shift_ref, bias_ref, decay_ref, skip_ref, gate_ref,
+):
+    grad_ref[...] = cot_ref[...].astype(F32) + part_ref[...].astype(F32)
+
+    @pl.when(pl.program_id(0) == 0)
+    def _():
+        inw_ref[...] = inw_in[...]
+        outw_ref[...] = outw_in[...]
+        norm_ref[...] = norm_in[0]
+        taps_ref[...] = sums_ref[:CONVK]
+        shift_ref[...] = sums_ref[CONVK]
+        bias_ref[...] = sums_ref[5, DI : DI + 128]
+        decay_ref[...] = sums_ref[5, DI + 128 :]
+        gate_ref[...] = sums_ref[5, :DI]
+        lane = lanes_of((1, 128))
+        total = jnp.zeros((1, 128), F32)
+        for h in range(HEADS):
+            here = jnp.sum(back_in[6:7, h * P_SIZE : (h + 1) * P_SIZE], axis=1, keepdims=True)
+            total = jnp.where(lane == h, here, total)
+        skip_ref[...] = total[0]
+
+
+def close(part, cotangent, inw, outw, sums, norm):
+    rows, width = part.shape
+    at = lambda i: (i, 0)
+    line = lambda n: pl.BlockSpec((n,), lambda i: (0,))
+    return pl.pallas_call(
+        close_kernel,
+        grid=(rows // Q,),
+        in_specs=[
+            spec((Q, width), at), spec((Q, width), at), whole(inw.shape), whole(outw.shape), whole(sums.shape),
+            whole(norm.shape), whole(sums.shape),
+        ],
+        out_specs=[
+            spec((Q, width), at), whole(inw.shape), whole(outw.shape), line(width), whole((CONVK, CH)), line(CH),
+            line(128), line(128), line(128), line(DI),
+        ],
+        out_shape=[
+            shaped((rows, width), F32), shaped(inw.shape, F32), shaped(outw.shape, F32), shaped((width,), F32),
+            shaped((CONVK, CH), F32), shaped((CH,), F32), shaped((128,), F32), shaped((128,), F32),
+            shaped((128,), F32), shaped((DI,), F32),
+        ],
+        compiler_params=params(),
+        name="close",
+    )(part, cotangent, inw, outw, sums, norm, sums)
 
 
 def local(
@@ -1362,26 +1496,26 @@
     rows, width = tokens.shape
     blocks = rows // Q
     near = lax.axis_size("ctx")
-    halo_tokens = lax.ppermute(
-        tokens[rows - 8 :], "ctx", [(k, k + 1) for k in range(near - 1)]
-    )
-    own_u = jnp.pad(in_weight[:, DI:], ((0, 0), (0, UW - (DPROJ - DI))))
-    own_z = in_weight[:, :DI]
     boxed = lax.axis_size("fsdp") == 8 and near == 4
     if boxed:
-        (w_u,) = gathered([own_u], 1)
-        later = [own_z, out_weight]
+        own = jnp.pad(in_weight, ((0, 0), (0, UW + DI - DPROJ)))
+        w_u, normed_more, turned = gathered(own, tokens, norm_gain.reshape(1, width), 1)
+        later = [own, out_weight]
+        later_widths = [DI, width]
     else:
-        w_u, w_z, w_o = [lax.all_gather(a, axes, axis=0, tiled=True) for a in (own_u, own_z, out_weight)]
+        own_u = jnp.pad(in_weight[:, DI:], ((0, 0), (0, UW - (DPROJ - DI))))
+        w_u, w_z, w_o = [
+            lax.all_gather(a, axes, axis=0, tiled=True) for a in (own_u, in_weight[:, :DI], out_weight)
+        ]
         later = []
+        later_widths = []
+        halo_tokens = lax.ppermute(tokens[rows - HALO :], "ctx", [(k, k + 1) for k in range(near - 1)])
+        wide = jnp.concatenate([tokens, halo_tokens], 0).astype(F32)
+        scale = lax.rsqrt(jnp.mean(wide * wide, axis=-1, keepdims=True) + epsilon)
+        normed_more = (wide * scale * norm_gain).astype(BF16)
     extra = len(later)
     anywhere = pl.BlockSpec(memory_space=pl.ANY)
 
-    def hats(values):
-        wide = values.astype(F32)
-        return wide * lax.rsqrt(jnp.mean(wide * wide, axis=-1, keepdims=True) + epsilon)
-
-    normed_more = (hats(jnp.concatenate([tokens, halo_tokens], 0)) * norm_gain).astype(BF16)
     normed = normed_more[:rows]
     valid = jnp.broadcast_to(valid_mask.astype(F32)[:, None], (rows, 128))
     keep = (1.0 - stretch_start[0].astype(F32)).reshape(1, 1)
@@ -1390,20 +1524,19 @@
     bias = jnp.pad(step_bias, (0, 128 - HEADS)).reshape(1, 128)
     logs = jnp.pad(decay_log, (0, 128 - HEADS)).reshape(1, 128)
     skips = jnp.repeat(skip_gain, P_SIZE).reshape(1, DI)
-    u = jnp.dot(normed_more, w_u, preferred_element_type=F32)
-    halo_block = rows // 8
 
     same = lambda c: (c, 0)
     same3 = lambda c: (c, 0, 0)
     one = lambda i: (jnp.minimum(i, blocks - 1), 0)
     one3 = lambda i: (jnp.minimum(i, blocks - 1), 0, 0)
     two = lambda i: (jnp.maximum(i - blocks, 0), 0)
-    val, vp, conv, bc, ssd, ent, logd, step, cum, start, *filled = pl.pallas_call(
+    val, vp, conv, bc, ssd, ent, logd, step, cum, start, u, ahead, *filled = pl.pallas_call(
         lambda *refs: forward_kernel(extra, *refs),
         grid=(2 * blocks,),
         in_specs=[
-            spec((Q, UW), one),
-            spec((8, UW), lambda c: (halo_block, 0)),
+            spec((Q, width), one),
+            spec((HALO, width), lambda c: (rows // HALO, 0)),
+            anywhere,
             spec((Q, 128), one),
             scalar(),
             whole((CONVK, CH)),
@@ -1424,6 +1557,8 @@
             spec((Q, 128), one),
             whole((blocks + 1, 8, DI)),
             whole((N, DI)),
+            spec((Q, UW), one),
+            whole((8, UW)),
         ]
         + [anywhere] * extra,
         out_shape=[
@@ -1437,8 +1572,10 @@
             shaped((rows, 128), F32),
             shaped((blocks + 1, 8, DI), F32),
             shaped((N, DI), BF16),
+            shaped((rows, UW), F32),
+            shaped((8, UW), F32),
         ]
-        + [shaped((32 * a.shape[0], a.shape[1]), a.dtype) for a in later],
+        + [shaped((32 * a.shape[0], n), a.dtype) for a, n in zip(later, later_widths)],
         scratch_shapes=[
             pltpu.VMEM((8, CH), F32),
             pltpu.VMEM((GROUPS, Q, 128), F32),
@@ -1453,12 +1590,16 @@
             pltpu.VMEM((N, DI), BF16),
             pltpu.VMEM((N, DI), BF16),
             pltpu.SemaphoreType.DMA((2,)),
+            pltpu.VMEM((w_u.shape[0], UW), BF16),
+            pltpu.SemaphoreType.DMA(()),
+            pltpu.VMEM((2, Q, GW), F32),
+            pltpu.VMEM((2, Q, GW), F32),
         ]
         + gather_scratch() * extra,
         compiler_params=params(2),
         cost_estimate=cost(15e9, 60e6),
         name="forward",
-    )(u, u, valid, keep, taps, shift, bias, logs, skips, *later)
+    )(normed_more, normed_more, w_u, valid, keep, taps, shift, bias, logs, skips, *later)
     if later:
         w_z, w_o = filled
 
@@ -1593,7 +1734,7 @@
             spec((Q, DI), back),
             spec((Q, CH), back),
             spec((Q, UW), back),
-            spec((8, UW), lambda i: (halo_block, 0)),
+            whole((8, UW)),
             spec((Q, 2 * N), back),
             spec((Q, 128), back),
             spec((Q, 128), back),
@@ -1642,29 +1783,32 @@
         cost_estimate=cost(15e9, 60e6),
         name="back",
     )(
-        keep, gin, gnext, entt, cum, vp, val, dvp, ds, conv, u, u, bc, logd, step, valid,
+        keep, gin, gnext, entt, cum, vp, val, dvp, ds, conv, u, ahead, bc, logd, step, valid,
         dlp, dlt, dbc, dc, taps, bias, logs, skips, *back_parts,
     )
     edge_back = lax.ppermute(edge, "ctx", [(k + 1, k) for k in range(near - 1)])
     du = lax.dynamic_update_slice(du, (last + edge_back).astype(BF16), (rows - 8, 0))
     if boxed:
         out_weight_grad, gate_columns = summed_gate
-        input_grad, in_weight_grad, sums = final(
-            normed.T, du, dz, tokens, cotangent, norm_gain.reshape(1, width), w_z, w_u, gate_columns, conv_sums,
+        part, in_weight_grad, sums, norm_sum = final(
+            turned, du, dz, tokens, norm_gain.reshape(1, width), w_z, w_u, gate_columns, conv_sums,
             gate_sums, small, 5,
         )
+        results = close(part, cotangent, in_weight_grad, out_weight_grad, sums, norm_sum)
+        input_grad, in_weight_grad, out_weight_grad, norm_sum, taps_sum, shift_sum = results[:6]
+        bias_sum, decay_sum, skip_sum, gate_sum = results[6:]
         return (
             output,
             input_grad,
             in_weight_grad,
             out_weight_grad,
-            sums[7, :width],
-            sums[:CONVK],
-            sums[CONVK],
-            sums[5, DI : DI + HEADS],
-            sums[5, DI + 128 : DI + 128 + HEADS],
-            jnp.sum(sums[6, :DI].reshape(HEADS, P_SIZE), axis=1),
-            sums[5, :DI],
+            norm_sum,
+            taps_sum,
+            shift_sum,
+            bias_sum[:HEADS],
+            decay_sum[:HEADS],
+            skip_sum[:HEADS],
+            gate_sum,
         )
     conv_columns = columns_of(normed, du)
     across = (((1,), (1,)), ((), ()))

time: 360 us -> 340 us (0.944)
  local copies, waits for them, and re-layouts: 24.6 us -> 6.6 us
  matrix products: 31.1 us -> 23.1 us
  Pallas kernels: 296 us -> 303 us
    pallas_call x1 -> x2, Pallas kernels: 33 us -> 43.2 us  [the longest x1 37.1 us: gathered(): pl.pallas_call(gather_kernel, in_specs=[anywhere, vmem, vmem], out_specs=...]
    unnamed x32 -> x6, local copies, waits for them, and re-layouts: 9.96 us -> 0.01 us
    dot_general x1 -> x0, matrix products: 8.24 us -> none  [local(): u = jnp.dot(normed_more, w_u, preferred_element_type=F32)]
    slice x9 -> x0, local copies, waits for them, and re-layouts: 7.51 us -> none  [the longest x1 1.53 us: local(): sums[5, :DI]]
    pallas_call x1, Pallas kernels: 56.7 us -> 52.2 us  [final(): pl.pallas_call(final_kernel, grid=(steps + blocks,), in_specs=[whole((wid...]
  transfers between devices with their start and end apart: 2 -> 1, of which waited for: 1 -> 1; matrix products, arithmetic and copies ran while one was open for 2% -> 0% of each run, Pallas kernels for 9% -> 0%
where the time goes in v1:
time: 340 us
  Pallas kernels  303 us (89%)
  matrix products  23.1 us (7%)
  local copies, waits for them, and re-layouts  6.6 us (2%)
    pallas_call x1, Pallas kernels, local(): pl.pallas_call(lambda *refs: forward_kernel(extra, *refs), grid=(2 * bloc...  63.5 us
    pallas_call x1, Pallas kernels, local(): pl.pallas_call(lambda *refs: back_kernel(len(back_parts), *refs), grid=(b...  53.4 us
    pallas_call x1, Pallas kernels, local(): pl.pallas_call(gate_kernel, grid=(blocks,), in_specs=[whole((N, DI)), spe...  53.4 us
    pallas_call x1, Pallas kernels, final(): pl.pallas_call(final_kernel, grid=(steps + blocks,), in_specs=[whole((wid...  52.2 us
    pallas_call x1, Pallas kernels, local(): pl.pallas_call(lambda *refs: mixing_kernel(len(mixing_parts), *refs), gri...  37.1 us
    pallas_call x1, Pallas kernels, gathered(): pl.pallas_call(gather_kernel, in_specs=[anywhere, vmem, vmem], out_specs=...  37.1 us
    dot_general x2, matrix products, columns_of(): lax.dot_general(left, right, (((0,), (0,)), ((), ())), preferred_element_...  14.9 us
    dot_general x1, matrix products, local(): z = jnp.dot(normed, w_z, preferred_element_type=F32).astype(BF16)  8.21 us
  transfers between devices with their start and end apart: 1, of which 1 were waited for; matrix products, arithmetic and copies ran while one was open for 0% of the time, Pallas kernels for 0%

profile of v1, /device:TPU:0, one launch (start us, length us, event | category | flops | bytes accessed | tf_op | source)
XLA Modules:
  0.0 339.8 jit_solution(10564776434006482850)
XLA Ops:
  1.3 0.7 convert_element_type.24
  2.0 1.3 reshape.54.refs_6_
  3.3 0.7 broadcast_in_dim.10
  4.0 0.7 reshape_reshape.3.refs_9_.refs_23_
  4.7 1.2 pad_bitcast_fusion
  5.9 1.7 pad.11.own.refs_10_
  7.6 37.1 %gather.1 = (bf16[1024,2432]{1,0:T(8,128)(2,1)}, bf16[1040,1024]{1,0:T(8,128)(2,1)}, bf16[1024,1024]{1,0:T(8,128)(2,1)}) custom-call(bf16[32,4480]{1,0:T(8,128)(2,1)} %pad.11.own.refs_10_, bf16[1024,1024]{1,0:T(8,128)(2,1)} %refs_4_.1, f32[1,1024]{1,0:T(1,128)} %bitcast.17), custom_call_target="tpu_custom_call" | custom-call | tf_op jit(solution)/shard_map/gather/pallas_call | solution.py:1001
  44.7 1.0 broadcast_in_dim.4.refs_3_.valid_ref.refs_15_
  45.7 0.0 copy-start
  45.7 63.5 %forward.1 = (bf16[1024,2048]{1,0:T(8,128)(2,1)}, bf16[1024,2048]{1,0:T(8,128)(2,1)}, bf16[1024,2304]{1,0:T(8,128)(2,1)}, bf16[1024,256]{1,0:T(8,128)(2,1)}, bf1...) custom-call(bf16[1040,1024]{1,0:T(8,128)(2,1)} %get-tuple-element.65, ...), custom_call_target="tpu_custom_call" | custom-call | flops 15000000512 | bytes 60000000 | tf_op jit(solution)/shard_map/forward/pallas_call | solution.py:1533
  109.1 0.0 copy-done
  109.2 8.2 %convolution_convert_fusion.2.z_ref = bf16[1024,2048]{1,0:T(8,128)(2,1)} fusion(bf16[1024,2048]{1,0:T(8,128)(2,1)} %get-tuple-element.70.refs_6_, bf16[1040,1024]{1,0:T(8,128)(2,1)S(1)} %copy-done), kind=kOutput, calls=%fused_computation.2 | convolution fusion | flops 4297064448 | bytes 10485760 | tf_op jit(solution)/shard_map/dot_general | solution.py:1606
  117.4 53.4 %gate.1 = (bf16[1024,1024]{1,0:T(8,128)(2,1)}, bf16[1024,2048]{1,0:T(8,128)(2,1)}, bf16[1024,1024]{1,0:T(8,128)(2,1)}, bf16[1024,2048]{1,0:T(8,128)(2,1)}, bf16[...) custom-call(bf16[128,2048]{1,0:T(8,128)(2,1)} %get-tuple-element.67., ...), custom_call_target="tpu_custom_call" | custom-call | flops 15000000512 | bytes 60000000 | tf_op jit(solution)/shard_map/gate/pallas_call | solution.py:1610
  170.8 0.0 copy-start.1
  170.8 0.0 copy-start.2
  170.8 8.7 %convolution_convert_fusion = bf16[1024,2048]{1,0:T(8,128)(2,1)} fusion(bf16[1024,2048]{1,0:T(8,128)(2,1)} %get-tuple-element.96.refs_2_, bf16[1040,1024]{1,0:T(8,128)(2,1)S(1)} %copy-done), kind=kOutput, calls=%fused_computation | convolution fusion | flops 4297064448 | bytes 10485760 | tf_op jit(solution)/shard_map/dot_general | solution.py:1673
  179.5 0.0 copy-done.1
  179.5 0.0 copy-done.2
  179.5 6.2 %convolution_convert_fusion.1 = bf16[2048,1024]{1,0:T(8,128)(2,1)} fusion(bf16[1024,2048]{1,0:T(8,128)(2,1)S(1)} %copy-done.1, bf16[1024,1024]{1,0:T(8,128)(2,1)S(1)} %copy-done.2), kind=kOutput, calls=%fused_computation.1 | convolution fusion | flops 4297064448 | bytes 10485760 | tf_op jit(solution)/shard_map/dot_general | solution.py:1673
  185.7 37.1 %mixing.1 = (bf16[1024,2048]{1,0:T(8,128)(2,1)}, f32[1024,256]{1,0:T(8,128)}, f32[1024,128]{1,0:T(8,128)}, bf16[128,2048]{1,0:T(8,128)(2,1)}, bf16[4,64,1024]{2,1,0:T(8,128)(2,1)}) custom-call(bf16[1024,2048]{1,0:T(8,128)(2,1)} %get-tuple-element.78.refs_0_.refs_8_, bf16[1024,2048]{1,0:T(8,128)(2,1)} %get-tuple-element.79.refs_1_.refs_5_, ...), custom_call_target="tpu_custom_call" | custom-call | flops 15000000512 | bytes 60000000 | tf_op jit(solution)/shard_map/mixing/pallas_call | solution.py:1684
  222.9 53.4 %back.1 = (bf16[1024,2432]{1,0:T(8,128)(2,1)}, f32[8,2304]{1,0:T(8,128)}, f32[8,2304]{1,0:T(8,128)}, f32[8,2304]{1,0:T(8,128)}, f32[8,128]{1,0:T(8,128)}, /*index=5*/f32[64,1024]{1,0:T(8,128)}, f32[32,2048]{1,0:T(8,128)}) custom-call(f32[1,1]{1,0:T(1,128)} %bitcast.1.refs_4_.refs_0_, bf16[128,2048]{1,0:T(8,128)(2,1)} %get-tuple-element.83.refs_1_, ...), custom_call_target="tpu_custom_call" | custom-call | flops 15000000512 | bytes 60000000 | tf_op jit(solution)/shard_map/back/pallas_call | solution.py:1722
  276.3 1.3 collective-permute-start
  277.6 2.1 collective-permute-done
  279.7 1.5 fusion.2.refs_1_.refs_3_
  281.2 52.2 %final.1 = (bf16[1024,1024]{1,0:T(8,128)(2,1)}, f32[32,4384]{1,0:T(8,128)}, f32[8,2304]{1,0:T(8,128)}, f32[1,1024]{1,0:T(1,128)}) custom-call(bf16[1024,1024]{1,0:T(8,128)(2,1)} %get-tuple-element.77.refs_0_, bf16[1024,2432]{1,0:T(8,128)(2,1)} %fusion.2.refs_1_.refs_3_, bf16[1024,2048]{1,0:T(8,128)(2,1)} %get-tuple-element.96.refs_2_, ...), custom_call_target="tpu_custom_call" | custom-call | flops 20000000000 | bytes 60000000 | tf_op jit(solution)/shard_map/final/pallas_call | solution.py:1382
  333.5 6.1 %close.1 = (f32[1024,1024]{1,0:T(8,128)}, f32[32,4384]{1,0:T(8,128)}, f32[64,1024]{1,0:T(8,128)}, f32[1024]{0:T(1024)}, f32[4,2304]{1,0:T(4,128)}, /*index=5*/f3...) custom-call(bf16[1024,1024]{1,0:T(8,128)(2,1)} %get-tuple-element.104.part_ref, ...), custom_call_target="tpu_custom_call" | custom-call | tf_op jit(solution)/shard_map/close/pallas_call | solution.py:1459
Async XLA Ops:
  45.7 63.5 %copy-start = (bf16[1040,1024]{1,0:T(8,128)(2,1)S(1)}, bf16[1040,1024]{1,0:T(8,128)(2,1)}, u32[]{:S(2)}) copy-start(bf16[1040,1024]{1,0:T(8,128)(2,1)} %get-tuple-element.65.refs_0_.refs_1_) | copy-start | bytes 6389764
  170.8 8.7 %copy-start.1 = (bf16[1024,2048]{1,0:T(8,128)(2,1)S(1)}, bf16[1024,2048]{1,0:T(8,128)(2,1)}, u32[]{:S(2)}) copy-start(bf16[1024,2048]{1,0:T(8,128)(2,1)} %get-tuple-element.81) | copy-start | bytes 12582916
  170.8 8.7 %copy-start.2 = (bf16[1024,1024]{1,0:T(8,128)(2,1)S(1)}, bf16[1024,1024]{1,0:T(8,128)(2,1)}, u32[]{:S(2)}) copy-start(bf16[1024,1024]{1,0:T(8,128)(2,1)} %get-tuple-element.82) | copy-start | bytes 6291460
  276.3 3.4 collective-permute-start

commit v2 on v1

--- a/solution.py
+++ b/solution.py
@@ -148,9 +148,22 @@
     )
 
 
+def lay_heads(out, line):
+    out[...] = jnp.zeros_like(out)
+    out[0, :HEADS] = line[...]
+
+
+def lay_out(out, line, picks):
+    shape = (8, 128)
+    heads = jnp.zeros((1, 128), F32)
+    for h in range(HEADS):
+        heads = jnp.where(lanes_of((1, 128)) == h, line[h], heads)
+    out[...] = nn(in_parts(jnp.broadcast_to(heads, shape)), picks[...])[0:1]
+
+
 def forward_kernel(count, *refs):
     (
-        normed_ref, halo_ref, wu_any, valid_ref, keep_ref, cw_ref, cb_ref, sb_ref, dl_ref, skip_ref,
+        normed_ref, halo_ref, wu_any, valid_ref, keep_ref, cw_ref, cb_line, sb_line, dl_line, skip_line,
     ) = refs[:10]
     own = refs[10 : 10 + count]
     (
@@ -158,9 +171,9 @@
     ) = refs[10 + count : 22 + count]
     outs = refs[22 + count : 22 + 2 * count]
     (
-        past, logs, picks, logt, inter, state, all_vp, all_val, all_bc, all_log, message, arrived, sems, wu, load, log_wide, step_wide,
-    ) = refs[22 + 2 * count : 39 + 2 * count]
-    gather_sems = refs[39 + 2 * count :]
+        past, logs, picks, logt, inter, state, all_vp, all_val, all_bc, all_log, message, arrived, sems, wu, load, log_wide, step_wide, cb_ref, sb_ref, dl_ref, skip_ref,
+    ) = refs[22 + 2 * count : 43 + 2 * count]
+    gather_sems = refs[43 + 2 * count :]
     i = pl.program_id(0)
     blocks = pl.num_programs(0) // 2
     first = i < blocks
@@ -180,6 +193,10 @@
         fetch = pltpu.make_async_copy(wu_any, wu, load)
         fetch.start()
         fill_picks(picks)
+        cb_ref[0] = cb_line[...]
+        lay_heads(sb_ref, sb_line)
+        lay_heads(dl_ref, dl_line)
+        lay_out(skip_ref, skip_line, picks)
         meet((box_peers() if count else []) + chain_peers())
         fetch.wait()
         before = nn(halo_ref[...], wu[...])[8:]
@@ -323,9 +340,9 @@
 
 def gate_kernel(
     start_ref, ssd_in, ent_ref, z_ref, val_ref, bc_ref, log_ref, cum_ref,
-    tok_ref, cot_ref, valid_ref, ow_ref, gain_ref,
+    tok_ref, cot_ref, valid_ref, ow_ref, gain_line,
     out_ref, gated_ref, bg_ref, ds_ref, dz_ref, entt_ref, gnext_ref, gout_ref, dlp_ref, dc_ref, sums_ref,
-    start, gstate, picks, ssd_s, mix_s, el_s, pe_s, gg_s, acc,
+    start, gstate, picks, ssd_s, mix_s, el_s, pe_s, gg_s, acc, gain_ref,
 ):
     i = pl.program_id(0)
     c = pl.num_programs(0) - 1 - i
@@ -334,6 +351,7 @@
     def _():
         start[...] = start_ref[...].astype(F32)
         fill_picks(picks)
+        gain_ref[0] = gain_line[...]
         gstate[...] = jnp.zeros_like(gstate)
         sums_ref[...] = jnp.zeros_like(sums_ref)
 
@@ -437,8 +455,8 @@
 FORWARD_HOPS = (0, 8, 20, 30)
 MIXING_HOPS = (0, 8, 20, 30)
 MIXING_PLACES = (0, 5, 12, 31)
-LINE_PLACES = (1, 4, 8, 12)
-BACK_PLACES = (0, 4, 9, 19, 22, 25, 28, 31)
+LINE_PLACES = (1, 12)
+BACK_PLACES = (0, 4, 9, 20, 31)
 
 
 def acting(places, acts):
@@ -450,14 +468,14 @@
 
 def plane_scratch(rows, columns):
     dma = pltpu.SemaphoreType.DMA
-    return scatter_scratch(rows, columns)[:6] + [dma((4,))] * 4
+    return scatter_scratch(rows, columns)[:6] + [dma((4,))] * 5
 
 
 def line_scratch(rows, columns):
     dma = pltpu.SemaphoreType.DMA
-    return [pltpu.VMEM((1, LINE, rows, columns), BF16)] + [pltpu.VMEM((LINE, rows, columns), BF16)] * 2 + [
-        dma((2, LINE))
-    ] * 2
+    return [
+        pltpu.VMEM((1, LINE, rows, columns), BF16), pltpu.VMEM((LINE, rows, columns), BF16), dma((LINE,)), dma((LINE,)),
+    ]
 
 
 def mixing_kernel(count, *refs):
@@ -475,7 +493,7 @@
     plan = []
     if count:
         held = refs[21 + 2 * count :]
-        part = Scatter(parts[0], None, *held[:6], None, None, tuple(held[6:10]) + (None, None))
+        part = Scatter(parts[0], None, *held[:6], None, tuple(held[6:10]) + (None, None), held[10])
         acts = [part.begin, part.corners, part.sides_out, lambda: part.hand_on(outs[0])]
         plan = acting(MIXING_PLACES, acts)
 
@@ -596,18 +614,18 @@
     (
         keep_ref, gin_ref, gnext_ref, entt_ref, cum_ref, vp_ref, val_ref, dvp_ref, ds_ref, conv_ref,
         u_ref, halo_ref, bc_ref, log_ref, step_ref, valid_ref, dlp_ref, dlt_ref, dbc_ref, dc_ref,
-        cw_ref, sb_ref, dl_ref, skip_ref,
+        cw_ref, sb_line, dl_line, skip_line,
     ) = refs[:24]
     parts = refs[24 : 24 + count]
     du_ref, last_ref, edge_ref, sums_ref, small_ref = refs[24 + count : 29 + count]
     outs = refs[29 + count : 29 + 2 * count]
-    gin, picks, head, epad, dlw, dst, drow = refs[29 + 2 * count : 36 + 2 * count]
+    gin, picks, head, epad, dlw, dst, drow, sb_ref, dl_ref, skip_ref = refs[29 + 2 * count : 39 + 2 * count]
     plan = []
     if count:
-        held = refs[36 + 2 * count :]
-        full = Scatter(parts[1], outs[1], *held[:8], held[8:14])
-        line = Scatter(None, outs[0], None, held[14], None, None, None, None, *held[15:17], (None,) * 4 + tuple(held[17:19]))
-        acts = [lambda: line.line(3), lambda: line.line(2), lambda: line.line(1), line.line_done]
+        held = refs[39 + 2 * count :]
+        full = Scatter(parts[1], outs[1], *held[:7], held[7:13], held[17])
+        line = Scatter(None, outs[0], None, held[13], None, None, None, None, held[14], (None,) * 4 + tuple(held[15:17]))
+        acts = [line.line, line.line_done]
         plan = acting(BACK_PLACES + LINE_PLACES, full.steps() + acts)
     i = pl.program_id(0)
     top = pl.num_programs(0)
@@ -616,10 +634,13 @@
     @pl.when(i == 0)
     def _():
         if count:
-            meet(box_peers())
+            meet(box_peers()[:3] + line_peers())
             line.kept[0] = parts[0][...]
         gin[...] = gin_ref[...].astype(F32)
         fill_picks(picks)
+        lay_heads(sb_ref, sb_line)
+        lay_heads(dl_ref, dl_line)
+        lay_out(skip_ref, skip_line, picks)
         head[...] = jnp.zeros_like(head)
         sums_ref[...] = jnp.zeros_like(sums_ref)
         small_ref[...] = jnp.zeros_like(small_ref)
@@ -779,6 +800,18 @@
     ]
 
 
+def plane_peers():
+    z, y, x, core = my_place()
+    turns = [(a, b, c) for a in range(2) for b in range(2) for c in range(2) if a + b + c]
+    return [(None, device_at(z, (y + a) % 2, (x + b) % 2, (core + c) % 2)) for a, b, c in turns]
+
+
+def line_peers():
+    z, y, x, core = my_place()
+    ups = [(z + r < LINE, device_at(z + r, y, x, core)) for r in range(1, LINE)]
+    return ups + [(z - r >= 0, device_at(z - r, y, x, core)) for r in range(1, LINE)]
+
+
 def meet(peers):
     barrier = pltpu.get_barrier_semaphore()
     count = 0
@@ -990,7 +1023,7 @@
     def _():
         halo.wait_send()
 
-    for at in range(parts + 1, len(lists[0]) + 1):
+    for at in range(parts + 1, len(lists[0]) + len(lists) - 1):
         hops(at)
 
 
@@ -1014,16 +1047,17 @@
 
 
 class Scatter:
-    def __init__(self, parts, out, got, kept, mixed_y, mixed_x, from_x, from_y, up, down, sems):
+    def __init__(self, parts, out, got, kept, mixed_y, mixed_x, from_x, from_y, along, sems, fetched=None):
         self.parts, self.out = parts, out
         self.got, self.kept = got, kept
         self.mixed = (mixed_y, mixed_x)
         self.sides = (from_x, from_y)
-        self.up, self.down = up, down
+        self.along = along
         self.twin_sent, self.twin_recv, self.sent, self.recv, self.line_sent, self.line_recv = sems
         self.place = my_place()
         self.rows = kept.shape[-2]
         self.last = kept.shape[0] - 1
+        self.fetched = fetched
 
     def groups(self):
         z, y, x, core = self.place
@@ -1037,9 +1071,19 @@
             (z, y, x, 1 - core),
         )
 
+    def fetch(self, k):
+        z, y, x, core = self.place
+        gy, gx = self.groups()[k]
+        return pltpu.make_async_copy(
+            self.parts.at[:, gy * 4 + gx * 2 + core], self.kept.at[k], self.fetched.at[k]
+        )
+
     def begin(self):
         for k in range(4):
             self.to_twin(k).start()
+        if self.fetched is not None:
+            for k in range(4):
+                self.fetch(k).start()
 
     def add(self, k, sources, first=0, rows=None):
         rows = self.rows if rows is None else rows
@@ -1065,9 +1109,11 @@
         z, y, x, core = self.place
         gy, gx = self.groups()[k]
         self.to_twin(k).wait_recv()
-        self.add(
-            k, [lambda b, at, here: self.parts[b, gy * 4 + gx * 2 + core, here], lambda b, at, here: self.got[k, b, here]]
-        )
+        mine = lambda b, at, here: self.parts[b, gy * 4 + gx * 2 + core, here]
+        if self.fetched is not None:
+            self.fetch(k).wait()
+            mine = self.own(k)
+        self.add(k, [mine, lambda b, at, here: self.got[k, b, here]])
 
     def corner_copy(self, half):
         z, y, x, core = self.place
@@ -1109,48 +1155,22 @@
             ],
         )
 
-    def line_copy(self, oz, way):
+    def line_copy(self, origin, target):
         z, y, x, core = self.place
-        buffer = self.up if way == 0 else self.down
-        peer = (z + 1, y, x, core) if way == 0 else (z - 1, y, x, core)
         return send(
-            self.kept.at[self.last, oz], buffer.at[oz], self.line_sent.at[way, oz], self.line_recv.at[way, oz], peer
+            self.kept.at[self.last, target], self.along.at[origin], self.line_sent.at[target],
+            self.line_recv.at[origin], (target, y, x, core),
         )
 
-    def add_line(self, oz, buffer):
-        def piece(n, unused):
-            here = pl.ds(pl.multiple_of(n * 16, 16), 16)
-            total = self.kept[self.last, oz, here].astype(F32) + buffer[oz, here].astype(F32)
-            self.kept[self.last, oz, here] = total.astype(BF16)
-            return unused
-
-        lax.fori_loop(0, self.rows // 16, piece, 0)
-
-    def line(self, r):
+    def others(self, act):
         z = self.place[0]
-
-        def upward():
-            oz = z + r
-
-            @pl.when(z > 0)
-            def _():
-                self.line_copy(oz, 0).wait_recv()
-                self.add_line(oz, self.up)
-
-            self.line_copy(oz, 0).start()
-
-        def downward():
-            oz = z - r
-
-            @pl.when(z < LINE - 1)
-            def _():
-                self.line_copy(oz, 1).wait_recv()
-                self.add_line(oz, self.down)
-
-            self.line_copy(oz, 1).start()
-
-        pl.when(z + r < LINE)(upward)
-        pl.when(z - r >= 0)(downward)
+        for r in range(1, LINE):
+            pl.when(z + r < LINE)(lambda r=r: act(z + r))
+            pl.when(z - r >= 0)(lambda r=r: act(z - r))
+
+    def line(self):
+        z = self.place[0]
+        self.others(lambda target: self.line_copy(z, target).start())
 
     def plane_sent(self):
         for k in range(4):
@@ -1169,19 +1189,12 @@
         z = self.place[0]
         self.out[...] = self.kept[self.last, z].astype(F32)
 
-        @pl.when(z > 0)
-        def _():
-            self.line_copy(z, 0).wait_recv()
-            self.out[...] += self.up[z].astype(F32)
-
-        @pl.when(z < LINE - 1)
-        def _():
-            self.line_copy(z, 1).wait_recv()
-            self.out[...] += self.down[z].astype(F32)
-
-        for r in range(1, LINE):
-            pl.when(z + r < LINE)(lambda r=r: self.line_copy(z + r, 0).wait_send())
-            pl.when(z - r >= 0)(lambda r=r: self.line_copy(z - r, 1).wait_send())
+        def arrive(origin):
+            self.line_copy(origin, z).wait_recv()
+            self.out[...] += self.along[origin].astype(F32)
+
+        self.others(arrive)
+        self.others(lambda target: self.line_copy(z, target).wait_send())
 
     def finish(self):
         self.line_done()
@@ -1189,8 +1202,7 @@
 
     def steps(self):
         return [
-            self.begin, self.corners, self.sides_out, self.sides_in, lambda: self.line(3), lambda: self.line(2),
-            lambda: self.line(1), self.finish,
+            self.begin, self.corners, self.sides_out, lambda: (self.sides_in(), self.line()), self.finish,
         ]
 
 
@@ -1205,9 +1217,68 @@
         pltpu.VMEM((LINE, rows, columns), BF16),
         pltpu.VMEM((LINE, rows, columns), BF16),
         pltpu.VMEM((LINE, rows, columns), BF16),
-        pltpu.VMEM((LINE, rows, columns), BF16),
-        dma((4,)), dma((4,)), dma((4,)), dma((4,)), dma((2, LINE)), dma((2, LINE)),
+        dma((4,)), dma((4,)), dma((4,)), dma((4,)), dma((LINE,)), dma((LINE,)),
     ]
+
+
+class Quick:
+    def __init__(self, own, out, plane, line, sems):
+        self.own, self.out, self.plane, self.along = own, out, plane, line
+        self.sent, self.recv, self.line_sent, self.line_recv = sems
+        self.place = my_place()
+
+    def peers(self):
+        z, y, x, core = self.place
+        turns = [(a, b, c) for a in range(2) for b in range(2) for c in range(2) if a + b + c]
+        return [((y + a) % 2, (x + b) % 2, (core + c) % 2) for a, b, c in turns]
+
+    def copy(self, origin, target):
+        z = self.place[0]
+        number = lambda where: where[0] * 4 + where[1] * 2 + where[2]
+        return send(
+            self.own, self.plane.at[number(origin)], self.sent.at[number(target)], self.recv.at[number(origin)],
+            (z,) + tuple(target),
+        )
+
+    def begin(self):
+        here = self.place[1:]
+        self.plane[here[0] * 4 + here[1] * 2 + here[2]] = self.own[...]
+        for peer in self.peers():
+            self.copy(here, peer).start()
+
+    def line_copy(self, origin, target):
+        z, y, x, core = self.place
+        return send(
+            self.along.at[z], self.along.at[origin], self.line_sent.at[target], self.line_recv.at[origin],
+            (target, y, x, core),
+        )
+
+    def others(self, act):
+        z = self.place[0]
+        for r in range(1, LINE):
+            pl.when(z + r < LINE)(lambda r=r: act(z + r))
+            pl.when(z - r >= 0)(lambda r=r: act(z - r))
+
+    def turn(self):
+        z, here = self.place[0], self.place[1:]
+        for peer in self.peers():
+            self.copy(peer, here).wait_recv()
+        total = self.plane[0]
+        for k in range(1, 8):
+            total = total + self.plane[k]
+        self.along[z] = total
+        self.others(lambda target: self.line_copy(z, target).start())
+
+    def finish(self):
+        z, here = self.place[0], self.place[1:]
+        self.others(lambda origin: self.line_copy(origin, z).wait_recv())
+        total = self.along[0]
+        for k in range(1, LINE):
+            total = total + self.along[k]
+        self.out[...] = total
+        for peer in self.peers():
+            self.copy(here, peer).wait_send()
+        self.others(lambda target: self.line_copy(z, target).wait_send())
 
 
 class Total:
@@ -1244,28 +1315,36 @@
         return [self.begin] + [lambda k=k: self.turn(k) for k in range(5)] + [self.finish]
 
 
-WIDE = 256
-SPLIT = 1280
+WIDE = 512
+SPLIT = 1536
+
+
+def patched(values, fixed, first):
+    count = values.shape[0]
+    end = values[count - 16 :].astype(F32)
+    own = jnp.logical_and(rows_of(end.shape) >= 8, lanes_of(end.shape) + first < CH)
+    chosen = jnp.where(own, fixed, end)
+    return jnp.concatenate([values[: count - 16], chosen.astype(BF16)], 0)
 
 
 def final_kernel(*refs):
     (
         turned_ref, du_cols, dz_ref, du_ref, tok_ref, gain_ref, wz_any, wu_any, gate_ref, conv_ref, gsum_ref,
-        small_ref,
-    ) = refs[:12]
-    grad_ref, inw_ref, sums_ref, norm_ref = refs[12:16]
+        small_ref, last_ref, edge_ref,
+    ) = refs[:14]
+    grad_ref, inw_ref, sums_ref, norm_ref = refs[14:18]
     (
         wz, wu, sems, parts_a, parts_b, out_a, out_b, packed, normed_grad, held, got, sent, recv, gains,
-        gains_held, gains_got, gains_sent, gains_recv,
-    ) = refs[16:34]
+        gains_plane, gains_line, gains_sent, gains_recv, gains_out, gains_in, fixed, edge_got, edge_sems, du_block,
+    ) = refs[18:42]
     i = pl.program_id(0)
     steps = pl.num_programs(0) - tok_blocks(turned_ref)
     z, y, x, core = my_place()
-    scr_a, scr_b = refs[34:48], refs[48:62]
-    sum_a = Scatter(parts_a, out_a, *scr_a[:8], scr_a[8:])
-    sum_b = Scatter(parts_b, out_b, *scr_b[:8], scr_b[8:])
+    scr_a, scr_b = refs[42:55], refs[55:68]
+    sum_a = Scatter(parts_a, out_a, *scr_a[:7], scr_a[7:])
+    sum_b = Scatter(parts_b, out_b, *scr_b[:7], scr_b[7:])
     small = Total(packed, sums_ref, held, got, sent, recv)
-    norm = Total(gains, norm_ref, gains_held, gains_got, gains_sent, gains_recv)
+    norm = Quick(gains, norm_ref, gains_plane, gains_line, (gains_sent, gains_recv, gains_out, gains_in))
     load_z = pltpu.make_async_copy(wz_any, wz, sems.at[0])
     load_u = pltpu.make_async_copy(wu_any, wu, sems.at[1])
 
@@ -1273,31 +1352,49 @@
     def _():
         load_z.start()
         load_u.start()
-        meet(box_peers() + [(None, device_at((z + 2) % LINE, y, x, core))])
+        meet(plane_peers() + line_peers() + chain_peers())
         packed[...] = jnp.zeros_like(packed)
         packed[0:5, :] = conv_ref[0:5, :]
         packed[5:6, :DI] = gsum_ref[0:1, :]
         packed[5:6, DI : DI + 128] = small_ref[0:1, :]
         packed[5:6, DI + 128 :] = small_ref[1:2, :]
         packed[6:7, :DI] = gsum_ref[1:2, :]
+        pos = lax.axis_index("ctx")
+        back_edge = pass_on(edge_ref, edge_got, edge_sems, -1)
+
+        @pl.when(pos > 0)
+        def _():
+            back_edge.start()
+
         gains[...] = jnp.zeros_like(gains)
         small.begin()
         inw_ref[:, :DI] = gate_ref[...]
+        fixed[...] = jnp.zeros_like(fixed)
+        fixed[8:16, :CH] = last_ref[...]
+
+        @pl.when(pos < lax.axis_size("ctx") - 1)
+        def _():
+            back_edge.wait_recv()
+            fixed[8:16, :CH] += edge_got[...]
+
+        @pl.when(pos > 0)
+        def _():
+            back_edge.wait_send()
 
     first = [
-        (8, lambda: small.turn(0)), (20, lambda: (sum_a.begin(), small.turn(1))), (28, sum_a.corners),
-        (36, lambda: (sum_a.sides_out(), small.turn(2))),
+        (4, lambda: small.turn(0)), (8, lambda: small.turn(1)), (12, lambda: (sum_a.begin(), small.turn(2))),
+        (16, lambda: (sum_a.corners(), small.turn(3))),
     ]
     second = [
-        (40, sum_b.begin), (43, sum_b.corners), (45, lambda: small.turn(3)),
-        (47, lambda: (sum_a.sides_in(), sum_a.line(3))), (49, sum_b.sides_out), (51, lambda: sum_a.line(2)),
-        (53, lambda: small.turn(4)), (55, lambda: sum_a.line(1)),
+        (20, lambda: (sum_b.begin(), sum_a.sides_out())), (23, sum_b.corners), (25, lambda: small.turn(4)),
+        (29, lambda: (sum_a.sides_in(), sum_a.line())), (30, sum_b.sides_out),
     ]
 
     @pl.when(i < steps)
     def _():
         when_at(4 * i, first)
-        result = nn(turned_ref[...], du_cols[...]).astype(BF16)
+        at = pl.ds(pl.multiple_of(i * WIDE, WIDE), WIDE)
+        result = nn(turned_ref[...], patched(du_cols[...], fixed[:, at], i * WIDE)).astype(BF16)
         rows = parts_a.shape[2]
 
         def keep(parts, cols, width):
@@ -1329,11 +1426,14 @@
     def _():
         width = tok_ref.shape[1]
         chunk = width // 4
+        at_end = i == pl.num_programs(0) - 1
+        du_block[:, :CH] = patched(du_ref[:, :CH], fixed[:, :CH], jnp.where(at_end, 0, CH))
+        du_block[:, CH:] = du_ref[:, CH:]
 
         def part(n, unused):
             when_at(4 * i + n, second)
             feats = pl.ds(pl.multiple_of(n * chunk, chunk), chunk)
-            normed_grad[:, feats] = nt(dz_ref[...], wz[feats, :]) + nt(du_ref[...], wu[feats, :])
+            normed_grad[:, feats] = nt(dz_ref[...], wz[feats, :]) + nt(du_block[...], wu[feats, :])
             return unused
 
         lax.fori_loop(0, 4, part, 0)
@@ -1350,18 +1450,12 @@
     def _():
         norm.begin()
         sum_b.sides_in()
-        sum_b.line(3)
-        norm.turn(0)
-        norm.turn(1)
-        sum_b.line(2)
-        norm.turn(2)
+        sum_b.line()
+        norm.turn()
         sum_a.finish()
-        sum_b.line(1)
-        norm.turn(3)
-        norm.turn(4)
+        norm.finish()
         sum_b.finish()
         small.finish()
-        norm.finish()
         inw_ref[:, DI : DI + SPLIT] = out_a[...]
         inw_ref[:, DI + SPLIT :] = out_b[:, : DPROJ - DI - SPLIT]
 
@@ -1370,7 +1464,7 @@
     return turned_ref.shape[1] // Q
 
 
-def final(turned, du, dz, tokens, gain, w_z, w_u, gate_columns, conv_sums, gate_sums, small, number):
+def final(turned, du, dz, tokens, gain, w_z, w_u, gate_columns, conv_sums, gate_sums, small, last, edge, number):
     width, rows = turned.shape
     steps = -(-UW // WIDE)
     blocks = rows // Q
@@ -1395,6 +1489,8 @@
             whole(sums),
             whole((8, DI)),
             whole((8, 128)),
+            whole((8, CH)),
+            whole((8, CH)),
         ],
         out_specs=[spec((Q, width), later), whole((own, DPROJ)), whole(sums), whole((1, width))],
         out_shape=[
@@ -1415,17 +1511,23 @@
             dma((5,)),
             dma((5,)),
             pltpu.VMEM((1, width), F32),
-            pltpu.VMEM((5, 1, width), F32),
-            pltpu.VMEM((5, 1, width), F32),
-            dma((5,)),
-            dma((5,)),
+            pltpu.VMEM((8, 1, width), F32),
+            pltpu.VMEM((LINE, 1, width), F32),
+            dma((8,)),
+            dma((8,)),
+            dma((LINE,)),
+            dma((LINE,)),
+            pltpu.VMEM((16, -(-UW // WIDE) * WIDE), F32),
+            pltpu.VMEM((8, CH), F32),
+            dma((2,)),
+            pltpu.VMEM((Q, UW), BF16),
         ]
         + scatter_scratch(own, SPLIT)
         + scatter_scratch(own, UW - SPLIT),
         compiler_params=params(number),
         cost_estimate=cost(20e9, 60e6),
         name="final",
-    )(turned, du, dz, du, tokens, gain, w_z, w_u, gate_columns, conv_sums, gate_sums, small)
+    )(turned, du, dz, du, tokens, gain, w_z, w_u, gate_columns, conv_sums, gate_sums, small, last, edge)
 
 
 def close_kernel(
@@ -1520,10 +1622,6 @@
     valid = jnp.broadcast_to(valid_mask.astype(F32)[:, None], (rows, 128))
     keep = (1.0 - stretch_start[0].astype(F32)).reshape(1, 1)
     taps = conv_weight
-    shift = conv_bias.reshape(1, CH)
-    bias = jnp.pad(step_bias, (0, 128 - HEADS)).reshape(1, 128)
-    logs = jnp.pad(decay_log, (0, 128 - HEADS)).reshape(1, 128)
-    skips = jnp.repeat(skip_gain, P_SIZE).reshape(1, DI)
 
     same = lambda c: (c, 0)
     same3 = lambda c: (c, 0, 0)
@@ -1540,10 +1638,10 @@
             spec((Q, 128), one),
             scalar(),
             whole((CONVK, CH)),
-            whole((1, CH)),
-            whole((1, 128)),
-            whole((1, 128)),
-            whole((1, DI)),
+            whole((CH,)),
+            whole((HEADS,)),
+            whole((HEADS,)),
+            scalar(),
         ]
         + [anywhere] * extra,
         out_specs=[
@@ -1594,19 +1692,22 @@
             pltpu.SemaphoreType.DMA(()),
             pltpu.VMEM((2, Q, GW), F32),
             pltpu.VMEM((2, Q, GW), F32),
+            pltpu.VMEM((1, CH), F32),
+            pltpu.VMEM((1, 128), F32),
+            pltpu.VMEM((1, 128), F32),
+            pltpu.VMEM((1, DI), F32),
         ]
         + gather_scratch() * extra,
         compiler_params=params(2),
         cost_estimate=cost(15e9, 60e6),
         name="forward",
-    )(normed_more, normed_more, w_u, valid, keep, taps, shift, bias, logs, skips, *later)
+    )(normed_more, normed_more, w_u, valid, keep, taps, conv_bias, step_bias, decay_log, skip_gain, *later)
     if later:
         w_z, w_o = filled
 
     z = jnp.dot(normed, w_z, preferred_element_type=F32).astype(BF16)
     back = lambda i: (blocks - 1 - i, 0)
     back3 = lambda i: (blocks - 1 - i, 0, 0)
-    gains = gate_gain.reshape(1, DI)
     output, gated, branch_grad, ds, dz, entt, gnext, gout, dlp, dc, gate_sums = pl.pallas_call(
         gate_kernel,
         grid=(blocks,),
@@ -1623,7 +1724,7 @@
             spec((Q, width), back),
             spec((Q, 128), back),
             whole((DI, width)),
-            whole((1, DI)),
+            whole((DI,)),
         ],
         out_specs=[
             spec((Q, width), back),
@@ -1661,12 +1762,13 @@
             pltpu.VMEM((Q, DI), F32),
             pltpu.VMEM((Q, DI), F32),
             pltpu.VMEM((Q, 128), F32),
+            pltpu.VMEM((1, DI), F32),
         ],
         compiler_params=params(),
         cost_estimate=cost(15e9, 60e6),
         name="gate",
     )(
-        start, ssd, ent, z, val, bc, logd, cum, tokens, cotangent, valid, w_o, gains,
+        start, ssd, ent, z, val, bc, logd, cum, tokens, cotangent, valid, w_o, gate_gain,
     )
 
     def columns_of(left, right):
@@ -1693,7 +1795,7 @@
             whole((N, DI)),
             whole((blocks + 1, 8, DI)),
         ]
-        + [pl.BlockSpec(memory_space=pltpu.VMEM) for a in mixing_parts],
+        + [anywhere for a in mixing_parts],
         out_specs=[spec((Q, DI), same), spec((Q, 2 * N), same), spec((Q, 128), same), whole((N, DI))]
         + [whole((LINE,) + a.shape[-2:]) for a in mixing_parts],
         out_shape=[
@@ -1744,11 +1846,11 @@
             spec((Q, 2 * N), back),
             spec((Q, N), back),
             whole((CONVK, CH)),
-            whole((1, 128)),
-            whole((1, 128)),
-            whole((1, DI)),
+            whole((HEADS,)),
+            whole((HEADS,)),
+            scalar(),
         ]
-        + [pl.BlockSpec(memory_space=pltpu.VMEM) for a in back_parts],
+        + [pl.BlockSpec(memory_space=pltpu.VMEM), anywhere][: len(back_parts)],
         out_specs=[
             spec((Q, UW), back),
             whole((8, CH)),
@@ -1773,9 +1875,14 @@
             pltpu.VMEM((Q, 128), F32),
             pltpu.VMEM((Q, 128), F32),
             pltpu.VMEM((16, 128), F32),
+            pltpu.VMEM((1, 128), F32),
+            pltpu.VMEM((1, 128), F32),
+            pltpu.VMEM((1, DI), F32),
         ]
         + (
-            scatter_scratch(*back_parts[1].shape[-2:]) + line_scratch(*back_parts[0].shape[-2:])
+            scatter_scratch(*back_parts[1].shape[-2:])
+            + line_scratch(*back_parts[0].shape[-2:])
+            + [pltpu.SemaphoreType.DMA((4,))]
             if back_parts
             else []
         ),
@@ -1784,15 +1891,13 @@
         name="back",
     )(
         keep, gin, gnext, entt, cum, vp, val, dvp, ds, conv, u, ahead, bc, logd, step, valid,
-        dlp, dlt, dbc, dc, taps, bias, logs, skips, *back_parts,
+        dlp, dlt, dbc, dc, taps, step_bias, decay_log, skip_gain, *back_parts,
     )
-    edge_back = lax.ppermute(edge, "ctx", [(k + 1, k) for k in range(near - 1)])
-    du = lax.dynamic_update_slice(du, (last + edge_back).astype(BF16), (rows - 8, 0))
     if boxed:
         out_weight_grad, gate_columns = summed_gate
         part, in_weight_grad, sums, norm_sum = final(
             turned, du, dz, tokens, norm_gain.reshape(1, width), w_z, w_u, gate_columns, conv_sums,
-            gate_sums, small, 5,
+            gate_sums, small, last, edge, 5,
         )
         results = close(part, cotangent, in_weight_grad, out_weight_grad, sums, norm_sum)
         input_grad, in_weight_grad, out_weight_grad, norm_sum, taps_sum, shift_sum = results[:6]
@@ -1810,6 +1915,8 @@
             skip_sum[:HEADS],
             gate_sum,
         )
+    edge_back = lax.ppermute(edge, "ctx", [(k + 1, k) for k in range(near - 1)])
+    du = lax.dynamic_update_slice(du, (last + edge_back).astype(BF16), (rows - 8, 0))
     conv_columns = columns_of(normed, du)
     across = (((1,), (1,)), ((), ()))
     normed_grad = lax.dot_general(dz, w_z, across, preferred_element_type=F32) + lax.dot_general(

time: 340 us -> 326 us (0.959)
  Pallas kernels: 303 us -> 297 us
  local copies, waits for them, and re-layouts: 6.6 us -> 2.7 us
    pallas_call x1, Pallas kernels: 53.4 us -> 49.7 us  [local(): pl.pallas_call(lambda *refs: back_kernel(len(back_parts), *refs), grid=(b...]
  transfers between devices with their start and end apart: 1 -> 0, of which waited for: 1 -> 0; matrix products, arithmetic and copies ran while one was open for 0% -> 0% of each run, Pallas kernels for 0% -> 0%
where the time goes in v2:
time: 326 us; the launch traced here: 325 us
  Pallas kernels  297 us (91%)
  matrix products  23.1 us (7%)
    pallas_call x1, Pallas kernels, local(): pl.pallas_call(lambda *refs: forward_kernel(extra, *refs), grid=(2 * bloc...  63.7 us
    pallas_call x1, Pallas kernels, local(): pl.pallas_call(gate_kernel, grid=(blocks,), in_specs=[whole((N, DI)), spe...  53.8 us
    pallas_call x1, Pallas kernels, final(): pl.pallas_call(final_kernel, grid=(steps + blocks,), in_specs=[whole((wid...  50.7 us
    pallas_call x1, Pallas kernels, local(): pl.pallas_call(lambda *refs: back_kernel(len(back_parts), *refs), grid=(b...  49.7 us
    pallas_call x1, Pallas kernels, gathered(): pl.pallas_call(gather_kernel, in_specs=[anywhere, vmem, vmem], out_specs=...  37.1 us
    pallas_call x1, Pallas kernels, local(): pl.pallas_call(lambda *refs: mixing_kernel(len(mixing_parts), *refs), gri...  36.2 us
    dot_general x2, matrix products, columns_of(): lax.dot_general(left, right, (((0,), (0,)), ((), ())), preferred_element_...  14.9 us
    dot_general x1, matrix products, local(): z = jnp.dot(normed, w_z, preferred_element_type=F32).astype(BF16)  8.21 us

profile of v2, /device:TPU:0, one launch (start us, length us, event | category | flops | bytes accessed | tf_op | source)
XLA Modules:
  0.0 325.4 jit_solution(2460674014373238087)
XLA Ops:
  1.3 0.7 convert_element_type.18
  2.0 1.7 pad.4.own.refs_10_
  3.7 1.0 broadcast_in_dim.2.refs_3_.valid_ref.refs_15_
  4.7 37.1 %gather.1 = (bf16[1024,2432]{1,0:T(8,128)(2,1)}, bf16[1040,1024]{1,0:T(8,128)(2,1)}, bf16[1024,1024]{1,0:T(8,128)(2,1)}) custom-call(bf16[32,4480]{1,0:T(8,128)(2,1)} %pad.4.own.refs_10_, bf16[1024,1024]{1,0:T(8,128)(2,1)} %refs_4_.1, f32[1,1024]{1,0:T(1,128)} %bitcast.12), custom_call_target="tpu_custom_call" | custom-call | tf_op jit(solution)/shard_map/gather/pallas_call | solution.py:1034
  41.8 0.0 copy-start
  41.8 63.7 %forward.1 = (bf16[1024,2048]{1,0:T(8,128)(2,1)}, bf16[1024,2048]{1,0:T(8,128)(2,1)}, bf16[1024,2304]{1,0:T(8,128)(2,1)}, bf16[1024,256]{1,0:T(8,128)(2,1)}, bf1...) custom-call(bf16[1040,1024]{1,0:T(8,128)(2,1)} %get-tuple-element.65, ...), custom_call_target="tpu_custom_call" | custom-call | flops 15000000512 | bytes 60000000 | tf_op jit(solution)/shard_map/forward/pallas_call | solution.py:1631
  105.5 0.0 copy-done
  105.5 8.2 %convolution_convert_fusion.2.z_ref = bf16[1024,2048]{1,0:T(8,128)(2,1)} fusion(bf16[1024,2048]{1,0:T(8,128)(2,1)} %get-tuple-element.70.refs_6_, bf16[1040,1024]{1,0:T(8,128)(2,1)S(1)} %copy-done), kind=kOutput, calls=%fused_computation.2 | convolution fusion | flops 4297064448 | bytes 10485760 | tf_op jit(solution)/shard_map/dot_general | solution.py:1708
  113.7 53.8 %gate.1 = (bf16[1024,1024]{1,0:T(8,128)(2,1)}, bf16[1024,2048]{1,0:T(8,128)(2,1)}, bf16[1024,1024]{1,0:T(8,128)(2,1)}, bf16[1024,2048]{1,0:T(8,128)(2,1)}, bf16[...) custom-call(bf16[128,2048]{1,0:T(8,128)(2,1)} %get-tuple-element.67., ...), custom_call_target="tpu_custom_call" | custom-call | flops 15000000512 | bytes 60000000 | tf_op jit(solution)/shard_map/gate/pallas_call | solution.py:1711
  167.5 0.0 copy-start.1
  167.5 0.0 copy-start.2
  167.5 8.7 %convolution_convert_fusion = bf16[1024,2048]{1,0:T(8,128)(2,1)} fusion(bf16[1024,2048]{1,0:T(8,128)(2,1)} %get-tuple-element.96.refs_2_, bf16[1040,1024]{1,0:T(8,128)(2,1)S(1)} %copy-done), kind=kOutput, calls=%fused_computation | convolution fusion | flops 4297064448 | bytes 10485760 | tf_op jit(solution)/shard_map/dot_general | solution.py:1775
  176.2 0.0 copy-done.1
  176.2 0.0 copy-done.2
  176.2 6.2 %convolution_convert_fusion.1 = bf16[2048,1024]{1,0:T(8,128)(2,1)} fusion(bf16[1024,2048]{1,0:T(8,128)(2,1)S(1)} %copy-done.1, bf16[1024,1024]{1,0:T(8,128)(2,1)S(1)} %copy-done.2), kind=kOutput, calls=%fused_computation.1 | convolution fusion | flops 4297064448 | bytes 10485760 | tf_op jit(solution)/shard_map/dot_general | solution.py:1775
  182.4 36.2 %mixing.1 = (bf16[1024,2048]{1,0:T(8,128)(2,1)}, f32[1024,256]{1,0:T(8,128)}, f32[1024,128]{1,0:T(8,128)}, bf16[128,2048]{1,0:T(8,128)(2,1)}, bf16[4,64,1024]{2,1,0:T(8,128)(2,1)}) custom-call(bf16[1024,2048]{1,0:T(8,128)(2,1)} %get-tuple-element.78.refs_0_.refs_8_, bf16[1024,2048]{1,0:T(8,128)(2,1)} %get-tuple-element.79.refs_1_.refs_5_, ...), custom_call_target="tpu_custom_call" | custom-call | flops 15000000512 | bytes 60000000 | tf_op jit(solution)/shard_map/mixing/pallas_call | solution.py:1786
  218.6 49.7 %back.1 = (bf16[1024,2432]{1,0:T(8,128)(2,1)}, f32[8,2304]{1,0:T(8,128)}, f32[8,2304]{1,0:T(8,128)}, f32[8,2304]{1,0:T(8,128)}, f32[8,128]{1,0:T(8,128)}, /*index=5*/f32[64,1024]{1,0:T(8,128)}, f32[32,2048]{1,0:T(8,128)}) custom-call(f32[1,1]{1,0:T(1,128)} %bitcast.1.refs_4_.refs_0_, bf16[128,2048]{1,0:T(8,128)(2,1)} %get-tuple-element.83.refs_1_, ...), custom_call_target="tpu_custom_call" | custom-call | flops 15000000512 | bytes 60000000 | tf_op jit(solution)/shard_map/back/pallas_call | solution.py:1824
  268.4 50.7 %final.1 = (bf16[1024,1024]{1,0:T(8,128)(2,1)}, f32[32,4384]{1,0:T(8,128)}, f32[8,2304]{1,0:T(8,128)}, f32[1,1024]{1,0:T(1,128)}) custom-call(bf16[1024,1024]{1,0:T(8,128)(2,1)} %get-tuple-element.77.refs_0_, bf16[1024,2432]{1,0:T(8,128)(2,1)} %get-tuple-element.97.refs_1_.refs_3_, bf16[1024,2048]{1,0:T(8,128)(2,1)} %get-tuple-element.96.refs_2_, ...), custom_call_target="tpu_custom_call" | custom-call | flops 20000000000 | bytes 60000000 | tf_op jit(solution)/shard_map/final/pallas_call | solution.py:1476
  319.1 6.1 %close.1 = (f32[1024,1024]{1,0:T(8,128)}, f32[32,4384]{1,0:T(8,128)}, f32[64,1024]{1,0:T(8,128)}, f32[1024]{0:T(1024)}, f32[4,2304]{1,0:T(4,128)}, /*index=5*/f3...) custom-call(bf16[1024,1024]{1,0:T(8,128)(2,1)} %get-tuple-element.104.part_ref, ...), custom_call_target="tpu_custom_call" | custom-call | tf_op jit(solution)/shard_map/close/pallas_call | solution.py:1561
Async XLA Ops:
  41.8 63.7 %copy-start = (bf16[1040,1024]{1,0:T(8,128)(2,1)S(1)}, bf16[1040,1024]{1,0:T(8,128)(2,1)}, u32[]{:S(2)}) copy-start(bf16[1040,1024]{1,0:T(8,128)(2,1)} %get-tuple-element.65.refs_0_.refs_1_) | copy-start | bytes 6389764
  167.5 8.7 %copy-start.1 = (bf16[1024,2048]{1,0:T(8,128)(2,1)S(1)}, bf16[1024,2048]{1,0:T(8,128)(2,1)}, u32[]{:S(2)}) copy-start(bf16[1024,2048]{1,0:T(8,128)(2,1)} %get-tuple-element.81) | copy-start | bytes 12582916
  167.5 8.7 %copy-start.2 = (bf16[1024,1024]{1,0:T(8,128)(2,1)S(1)}, bf16[1024,1024]{1,0:T(8,128)(2,1)}, u32[]{:S(2)}) copy-start(bf16[1024,1024]{1,0:T(8,128)(2,1)} %get-tuple-element.82) | copy-start | bytes 6291460

commit v3 on v2

--- a/solution.py
+++ b/solution.py
@@ -340,15 +340,16 @@
 
 def gate_kernel(
     start_ref, ssd_in, ent_ref, z_ref, val_ref, bc_ref, log_ref, cum_ref,
-    tok_ref, cot_ref, valid_ref, ow_ref, gain_line,
+    tok_ref, cot_ref, valid_ref, ow_any, gain_line,
     out_ref, gated_ref, bg_ref, ds_ref, dz_ref, entt_ref, gnext_ref, gout_ref, dlp_ref, dc_ref, sums_ref,
-    start, gstate, picks, ssd_s, mix_s, el_s, pe_s, gg_s, acc, gain_ref,
+    start, gstate, picks, ssd_s, mix_s, el_s, pe_s, gg_s, acc, gain_ref, ow_ref, load,
 ):
     i = pl.program_id(0)
     c = pl.num_programs(0) - 1 - i
 
     @pl.when(i == 0)
     def _():
+        pltpu.make_async_copy(ow_any, ow_ref, load).start()
         start[...] = start_ref[...].astype(F32)
         fill_picks(picks)
         gain_ref[0] = gain_line[...]
@@ -383,6 +384,11 @@
         return unused
 
     lax.fori_loop(0, GROUPS, enter, 0)
+
+    @pl.when(i == 0)
+    def _():
+        pltpu.make_async_copy(ow_any, ow_ref, load).wait()
+
     inv = lax.rsqrt(jnp.sum(acc[...], axis=1, keepdims=True) * (1.0 / DI) + epsilon)
     inv = jnp.broadcast_to(inv, (Q, 128))
     valid = valid_ref[...]
@@ -1316,7 +1322,7 @@
 
 
 WIDE = 512
-SPLIT = 1536
+PIECES = ((0, 1024), (1024, 1024), (2048, UW - 2048))
 
 
 def patched(values, fixed, first):
@@ -1334,15 +1340,16 @@
     ) = refs[:14]
     grad_ref, inw_ref, sums_ref, norm_ref = refs[14:18]
     (
-        wz, wu, sems, parts_a, parts_b, out_a, out_b, packed, normed_grad, held, got, sent, recv, gains,
+        wz, wu, sems, parts_a, parts_b, parts_c, out_a, out_b, out_c, packed, normed_grad, held, got, sent, recv, gains,
         gains_plane, gains_line, gains_sent, gains_recv, gains_out, gains_in, fixed, edge_got, edge_sems, du_block,
-    ) = refs[18:42]
+    ) = refs[18:44]
     i = pl.program_id(0)
     steps = pl.num_programs(0) - tok_blocks(turned_ref)
     z, y, x, core = my_place()
-    scr_a, scr_b = refs[42:55], refs[55:68]
+    scr_a, scr_b, scr_c = refs[44:57], refs[57:70], refs[70:83]
     sum_a = Scatter(parts_a, out_a, *scr_a[:7], scr_a[7:])
     sum_b = Scatter(parts_b, out_b, *scr_b[:7], scr_b[7:])
+    sum_c = Scatter(parts_c, out_c, *scr_c[:7], scr_c[7:])
     small = Total(packed, sums_ref, held, got, sent, recv)
     norm = Quick(gains, norm_ref, gains_plane, gains_line, (gains_sent, gains_recv, gains_out, gains_in))
     load_z = pltpu.make_async_copy(wz_any, wz, sems.at[0])
@@ -1382,12 +1389,12 @@
             back_edge.wait_send()
 
     first = [
-        (4, lambda: small.turn(0)), (8, lambda: small.turn(1)), (12, lambda: (sum_a.begin(), small.turn(2))),
-        (16, lambda: (sum_a.corners(), small.turn(3))),
+        (8, lambda: (sum_a.begin(), small.turn(0))), (12, sum_a.corners), (16, lambda: (sum_b.begin(), small.turn(1))),
     ]
     second = [
-        (20, lambda: (sum_b.begin(), sum_a.sides_out())), (23, sum_b.corners), (25, lambda: small.turn(4)),
-        (29, lambda: (sum_a.sides_in(), sum_a.line())), (30, sum_b.sides_out),
+        (20, lambda: (sum_a.sides_out(), sum_c.begin())), (22, sum_b.corners), (23, lambda: small.turn(2)),
+        (24, sum_c.corners), (26, lambda: small.turn(3)), (28, sum_b.sides_out),
+        (29, lambda: (sum_a.sides_in(), sum_a.line())), (30, lambda: small.turn(4)), (31, sum_c.sides_out),
     ]
 
     @pl.when(i < steps)
@@ -1403,19 +1410,13 @@
                     first = (b * 8 + q) * rows
                     parts[b, q, :, cols] = result[first : first + rows, :width]
 
-        edge = SPLIT // WIDE
-
-        @pl.when(i < edge)
-        def _():
-            keep(parts_a, pl.ds(pl.multiple_of(i * WIDE, WIDE), WIDE), WIDE)
-
-        @pl.when(jnp.logical_and(i >= edge, i < steps - 1))
-        def _():
-            keep(parts_b, pl.ds(pl.multiple_of((i - edge) * WIDE, WIDE), WIDE), WIDE)
-
-        @pl.when(i == steps - 1)
-        def _():
-            keep(parts_b, slice((steps - 1 - edge) * WIDE, UW - SPLIT), UW - SPLIT - (steps - 1 - edge) * WIDE)
+        for parts, (begin, count) in zip((parts_a, parts_b, parts_c), PIECES):
+            for at in range(0, count, WIDE):
+                wide = min(WIDE, count - at)
+
+                @pl.when(i == (begin + at) // WIDE)
+                def _(parts=parts, at=at, wide=wide):
+                    keep(parts, slice(at, at + wide), wide)
 
     @pl.when(i == steps)
     def _():
@@ -1452,12 +1453,16 @@
         sum_b.sides_in()
         sum_b.line()
         norm.turn()
+        sum_c.sides_in()
+        sum_c.line()
         sum_a.finish()
         norm.finish()
         sum_b.finish()
+        sum_c.finish()
         small.finish()
-        inw_ref[:, DI : DI + SPLIT] = out_a[...]
-        inw_ref[:, DI + SPLIT :] = out_b[:, : DPROJ - DI - SPLIT]
+        for out, (begin, count) in zip((out_a, out_b, out_c), PIECES):
+            count = min(count, DPROJ - DI - begin)
+            inw_ref[:, DI + begin : DI + begin + count] = out[:, :count]
 
 
 def tok_blocks(turned_ref):
@@ -1500,10 +1505,8 @@
             pltpu.VMEM((width, DI), BF16),
             pltpu.VMEM((width, UW), BF16),
             dma((2,)),
-            pltpu.VMEM((LINE, 8, own, SPLIT), BF16),
-            pltpu.VMEM((LINE, 8, own, UW - SPLIT), BF16),
-            pltpu.VMEM((own, SPLIT), F32),
-            pltpu.VMEM((own, UW - SPLIT), F32),
+            *[pltpu.VMEM((LINE, 8, own, count), BF16) for begin, count in PIECES],
+            *[pltpu.VMEM((own, count), F32) for begin, count in PIECES],
             pltpu.VMEM(sums, F32),
             pltpu.VMEM((Q, width), F32),
             pltpu.VMEM((5,) + sums, F32),
@@ -1522,8 +1525,7 @@
             dma((2,)),
             pltpu.VMEM((Q, UW), BF16),
         ]
-        + scatter_scratch(own, SPLIT)
-        + scatter_scratch(own, UW - SPLIT),
+        + [each for begin, count in PIECES for each in scatter_scratch(own, count)],
         compiler_params=params(number),
         cost_estimate=cost(20e9, 60e6),
         name="final",
@@ -1723,7 +1725,7 @@
             spec((Q, width), back),
             spec((Q, width), back),
             spec((Q, 128), back),
-            whole((DI, width)),
+            anywhere,
             whole((DI,)),
         ],
         out_specs=[
@@ -1763,6 +1765,8 @@
             pltpu.VMEM((Q, DI), F32),
             pltpu.VMEM((Q, 128), F32),
             pltpu.VMEM((1, DI), F32),
+            pltpu.VMEM((DI, width), BF16),
+            pltpu.SemaphoreType.DMA(()),
         ],
         compiler_params=params(),
         cost_estimate=cost(15e9, 60e6),

time: 326 us -> 322 us (0.988)
  no operation moved by 1% of the time
where the time goes in v3:
time: 322 us
  Pallas kernels  294 us (91%)
  matrix products  23.1 us (7%)
    pallas_call x1, Pallas kernels, local(): pl.pallas_call(lambda *refs: forward_kernel(extra, *refs), grid=(2 * bloc...  63.7 us
    pallas_call x1, Pallas kernels, local(): pl.pallas_call(gate_kernel, grid=(blocks,), in_specs=[whole((N, DI)), spe...  52.7 us
    pallas_call x1, Pallas kernels, local(): pl.pallas_call(lambda *refs: back_kernel(len(back_parts), *refs), grid=(b...  49.7 us
    pallas_call x1, Pallas kernels, final(): pl.pallas_call(final_kernel, grid=(steps + blocks,), in_specs=[whole((wid...  48.2 us
    pallas_call x1, Pallas kernels, gathered(): pl.pallas_call(gather_kernel, in_specs=[anywhere, vmem, vmem], out_specs=...  37.1 us
    pallas_call x1, Pallas kernels, local(): pl.pallas_call(lambda *refs: mixing_kernel(len(mixing_parts), *refs), gri...  36.2 us
    dot_general x2, matrix products, columns_of(): lax.dot_general(left, right, (((0,), (0,)), ((), ())), preferred_element_...  14.9 us
    dot_general x1, matrix products, local(): z = jnp.dot(normed, w_z, preferred_element_type=F32).astype(BF16)  8.21 us

profile of v3, /device:TPU:0, one launch (start us, length us, event | category | flops | bytes accessed | tf_op | source)
XLA Modules:
  0.0 321.9 jit_solution(14802803047900085333)
XLA Ops:
  1.3 0.7 convert_element_type.18
  2.0 1.7 pad.4.own.refs_10_
  3.7 1.0 broadcast_in_dim.2.refs_3_.valid_ref.refs_15_
  4.7 37.1 %gather.1 = (bf16[1024,2432]{1,0:T(8,128)(2,1)}, bf16[1040,1024]{1,0:T(8,128)(2,1)}, bf16[1024,1024]{1,0:T(8,128)(2,1)}) custom-call(bf16[32,4480]{1,0:T(8,128)(2,1)} %pad.4.own.refs_10_, bf16[1024,1024]{1,0:T(8,128)(2,1)} %refs_4_.1, f32[1,1024]{1,0:T(1,128)} %bitcast.12), custom_call_target="tpu_custom_call" | custom-call | tf_op jit(solution)/shard_map/gather/pallas_call | solution.py:1040
  41.8 0.0 copy-start
  41.8 63.7 %forward.1 = (bf16[1024,2048]{1,0:T(8,128)(2,1)}, bf16[1024,2048]{1,0:T(8,128)(2,1)}, bf16[1024,2304]{1,0:T(8,128)(2,1)}, bf16[1024,256]{1,0:T(8,128)(2,1)}, bf1...) custom-call(bf16[1040,1024]{1,0:T(8,128)(2,1)} %get-tuple-element.65, ...), custom_call_target="tpu_custom_call" | custom-call | flops 15000000512 | bytes 60000000 | tf_op jit(solution)/shard_map/forward/pallas_call | solution.py:1633
  105.5 0.0 copy-done
  105.5 8.2 %convolution_convert_fusion.2.z_ref = bf16[1024,2048]{1,0:T(8,128)(2,1)} fusion(bf16[1024,2048]{1,0:T(8,128)(2,1)} %get-tuple-element.70.refs_6_, bf16[1040,1024]{1,0:T(8,128)(2,1)S(1)} %copy-done), kind=kOutput, calls=%fused_computation.2 | convolution fusion | flops 4297064448 | bytes 10485760 | tf_op jit(solution)/shard_map/dot_general | solution.py:1710
  113.7 52.7 %gate.1 = (bf16[1024,1024]{1,0:T(8,128)(2,1)}, bf16[1024,2048]{1,0:T(8,128)(2,1)}, bf16[1024,1024]{1,0:T(8,128)(2,1)}, bf16[1024,2048]{1,0:T(8,128)(2,1)}, bf16[...) custom-call(bf16[128,2048]{1,0:T(8,128)(2,1)} %get-tuple-element.67., ...), custom_call_target="tpu_custom_call" | custom-call | flops 15000000512 | bytes 60000000 | tf_op jit(solution)/shard_map/gate/pallas_call | solution.py:1713
  166.4 0.0 copy-start.1
  166.4 0.0 copy-start.2
  166.5 8.7 %convolution_convert_fusion = bf16[1024,2048]{1,0:T(8,128)(2,1)} fusion(bf16[1024,2048]{1,0:T(8,128)(2,1)} %get-tuple-element.96.refs_2_, bf16[1040,1024]{1,0:T(8,128)(2,1)S(1)} %copy-done), kind=kOutput, calls=%fused_computation | convolution fusion | flops 4297064448 | bytes 10485760 | tf_op jit(solution)/shard_map/dot_general | solution.py:1779
  175.1 0.0 copy-done.1
  175.1 0.0 copy-done.2
  175.1 6.2 %convolution_convert_fusion.1 = bf16[2048,1024]{1,0:T(8,128)(2,1)} fusion(bf16[1024,2048]{1,0:T(8,128)(2,1)S(1)} %copy-done.1, bf16[1024,1024]{1,0:T(8,128)(2,1)S(1)} %copy-done.2), kind=kOutput, calls=%fused_computation.1 | convolution fusion | flops 4297064448 | bytes 10485760 | tf_op jit(solution)/shard_map/dot_general | solution.py:1779
  181.3 36.2 %mixing.1 = (bf16[1024,2048]{1,0:T(8,128)(2,1)}, f32[1024,256]{1,0:T(8,128)}, f32[1024,128]{1,0:T(8,128)}, bf16[128,2048]{1,0:T(8,128)(2,1)}, bf16[4,64,1024]{2,1,0:T(8,128)(2,1)}) custom-call(bf16[1024,2048]{1,0:T(8,128)(2,1)} %get-tuple-element.78.refs_0_.refs_8_, bf16[1024,2048]{1,0:T(8,128)(2,1)} %get-tuple-element.79.refs_1_.refs_5_, ...), custom_call_target="tpu_custom_call" | custom-call | flops 15000000512 | bytes 60000000 | tf_op jit(solution)/shard_map/mixing/pallas_call | solution.py:1790
  217.6 49.7 %back.1 = (bf16[1024,2432]{1,0:T(8,128)(2,1)}, f32[8,2304]{1,0:T(8,128)}, f32[8,2304]{1,0:T(8,128)}, f32[8,2304]{1,0:T(8,128)}, f32[8,128]{1,0:T(8,128)}, /*index=5*/f32[64,1024]{1,0:T(8,128)}, f32[32,2048]{1,0:T(8,128)}) custom-call(f32[1,1]{1,0:T(1,128)} %bitcast.1.refs_4_.refs_0_, bf16[128,2048]{1,0:T(8,128)(2,1)} %get-tuple-element.83.refs_1_, ...), custom_call_target="tpu_custom_call" | custom-call | flops 15000000512 | bytes 60000000 | tf_op jit(solution)/shard_map/back/pallas_call | solution.py:1828
  267.3 48.2 %final.1 = (bf16[1024,1024]{1,0:T(8,128)(2,1)}, f32[32,4384]{1,0:T(8,128)}, f32[8,2304]{1,0:T(8,128)}, f32[1,1024]{1,0:T(1,128)}) custom-call(bf16[1024,1024]{1,0:T(8,128)(2,1)} %get-tuple-element.77.refs_0_, bf16[1024,2432]{1,0:T(8,128)(2,1)} %get-tuple-element.97.refs_1_.refs_3_, bf16[1024,2048]{1,0:T(8,128)(2,1)} %get-tuple-element.96.refs_2_, ...), custom_call_target="tpu_custom_call" | custom-call | flops 20000000000 | bytes 60000000 | tf_op jit(solution)/shard_map/final/pallas_call | solution.py:1481
  315.6 6.1 %close.1 = (f32[1024,1024]{1,0:T(8,128)}, f32[32,4384]{1,0:T(8,128)}, f32[64,1024]{1,0:T(8,128)}, f32[1024]{0:T(1024)}, f32[4,2304]{1,0:T(4,128)}, /*index=5*/f3...) custom-call(bf16[1024,1024]{1,0:T(8,128)(2,1)} %get-tuple-element.104.part_ref, ...), custom_call_target="tpu_custom_call" | custom-call | tf_op jit(solution)/shard_map/close/pallas_call | solution.py:1563
Async XLA Ops:
  41.8 63.7 %copy-start = (bf16[1040,1024]{1,0:T(8,128)(2,1)S(1)}, bf16[1040,1024]{1,0:T(8,128)(2,1)}, u32[]{:S(2)}) copy-start(bf16[1040,1024]{1,0:T(8,128)(2,1)} %get-tuple-element.65.refs_0_.refs_1_) | copy-start | bytes 6389764
  166.4 8.7 %copy-start.1 = (bf16[1024,2048]{1,0:T(8,128)(2,1)S(1)}, bf16[1024,2048]{1,0:T(8,128)(2,1)}, u32[]{:S(2)}) copy-start(bf16[1024,2048]{1,0:T(8,128)(2,1)} %get-tuple-element.81) | copy-start | bytes 12582916
  166.4 8.7 %copy-start.2 = (bf16[1024,1024]{1,0:T(8,128)(2,1)S(1)}, bf16[1024,1024]{1,0:T(8,128)(2,1)}, u32[]{:S(2)}) copy-start(bf16[1024,1024]{1,0:T(8,128)(2,1)} %get-tuple-element.82) | copy-start | bytes 6291460

commit v4 on v3

--- a/solution.py
+++ b/solution.py
@@ -457,12 +457,12 @@
         gout_ref[...] = gstate[...].astype(BF16)
 
 
-FORWARD_PLACES = tuple(5 * k for k in range(13))
+FORWARD_PLACES = (0, 3, 7, 11, 16, 21, 26, 31, 36, 41, 47, 53, 63)
 FORWARD_HOPS = (0, 8, 20, 30)
-MIXING_HOPS = (0, 8, 20, 30)
+MIXING_HOPS = (0, 6, 18, 28)
 MIXING_PLACES = (0, 5, 12, 31)
 LINE_PLACES = (1, 12)
-BACK_PLACES = (0, 4, 9, 20, 31)
+BACK_PLACES = (0, 3, 8, 19, 30)
 
 
 def acting(places, acts):

time: 322 us -> 322 us (level)
  no operation moved by 1% of the time
where the time goes in v4:
time: 322 us; the launch traced here: 321 us
  Pallas kernels  293 us (91%)
  matrix products  23.1 us (7%)
    pallas_call x1, Pallas kernels, local(): pl.pallas_call(lambda *refs: forward_kernel(extra, *refs), grid=(2 * bloc...  61.5 us
    pallas_call x1, Pallas kernels, local(): pl.pallas_call(gate_kernel, grid=(blocks,), in_specs=[whole((N, DI)), spe...  52.7 us
    pallas_call x1, Pallas kernels, local(): pl.pallas_call(lambda *refs: back_kernel(len(back_parts), *refs), grid=(b...  51.8 us
    pallas_call x1, Pallas kernels, final(): pl.pallas_call(final_kernel, grid=(steps + blocks,), in_specs=[whole((wid...  48.1 us
    pallas_call x1, Pallas kernels, gathered(): pl.pallas_call(gather_kernel, in_specs=[anywhere, vmem, vmem], out_specs=...  37.1 us
    pallas_call x1, Pallas kernels, local(): pl.pallas_call(lambda *refs: mixing_kernel(len(mixing_parts), *refs), gri...  35.8 us
    dot_general x2, matrix products, columns_of(): lax.dot_general(left, right, (((0,), (0,)), ((), ())), preferred_element_...  14.9 us
    dot_general x1, matrix products, local(): z = jnp.dot(normed, w_z, preferred_element_type=F32).astype(BF16)  8.21 us

profile of v4, /device:TPU:0, one launch (start us, length us, event | category | flops | bytes accessed | tf_op | source)
XLA Modules:
  0.0 321.2 jit_solution(4246086493923006902)
XLA Ops:
  1.3 0.7 convert_element_type.18
  2.0 1.7 pad.4.own.refs_10_
  3.7 1.0 broadcast_in_dim.2.refs_3_.valid_ref.refs_15_
  4.7 37.1 %gather.1 = (bf16[1024,2432]{1,0:T(8,128)(2,1)}, bf16[1040,1024]{1,0:T(8,128)(2,1)}, bf16[1024,1024]{1,0:T(8,128)(2,1)}) custom-call(bf16[32,4480]{1,0:T(8,128)(2,1)} %pad.4.own.refs_10_, bf16[1024,1024]{1,0:T(8,128)(2,1)} %refs_4_.1, f32[1,1024]{1,0:T(1,128)} %bitcast.12), custom_call_target="tpu_custom_call" | custom-call | tf_op jit(solution)/shard_map/gather/pallas_call | solution.py:1040
  41.8 0.0 copy-start
  41.8 61.5 %forward.1 = (bf16[1024,2048]{1,0:T(8,128)(2,1)}, bf16[1024,2048]{1,0:T(8,128)(2,1)}, bf16[1024,2304]{1,0:T(8,128)(2,1)}, bf16[1024,256]{1,0:T(8,128)(2,1)}, bf1...) custom-call(bf16[1040,1024]{1,0:T(8,128)(2,1)} %get-tuple-element.65, ...), custom_call_target="tpu_custom_call" | custom-call | flops 15000000512 | bytes 60000000 | tf_op jit(solution)/shard_map/forward/pallas_call | solution.py:1633
  103.3 0.0 copy-done
  103.3 8.2 %convolution_convert_fusion.2.z_ref = bf16[1024,2048]{1,0:T(8,128)(2,1)} fusion(bf16[1024,2048]{1,0:T(8,128)(2,1)} %get-tuple-element.70.refs_6_, bf16[1040,1024]{1,0:T(8,128)(2,1)S(1)} %copy-done), kind=kOutput, calls=%fused_computation.2 | convolution fusion | flops 4297064448 | bytes 10485760 | tf_op jit(solution)/shard_map/dot_general | solution.py:1710
  111.5 52.7 %gate.1 = (bf16[1024,1024]{1,0:T(8,128)(2,1)}, bf16[1024,2048]{1,0:T(8,128)(2,1)}, bf16[1024,1024]{1,0:T(8,128)(2,1)}, bf16[1024,2048]{1,0:T(8,128)(2,1)}, bf16[...) custom-call(bf16[128,2048]{1,0:T(8,128)(2,1)} %get-tuple-element.67., ...), custom_call_target="tpu_custom_call" | custom-call | flops 15000000512 | bytes 60000000 | tf_op jit(solution)/shard_map/gate/pallas_call | solution.py:1713
  164.3 0.0 copy-start.1
  164.3 0.0 copy-start.2
  164.3 8.7 %convolution_convert_fusion = bf16[1024,2048]{1,0:T(8,128)(2,1)} fusion(bf16[1024,2048]{1,0:T(8,128)(2,1)} %get-tuple-element.96.refs_2_, bf16[1040,1024]{1,0:T(8,128)(2,1)S(1)} %copy-done), kind=kOutput, calls=%fused_computation | convolution fusion | flops 4297064448 | bytes 10485760 | tf_op jit(solution)/shard_map/dot_general | solution.py:1779
  173.0 0.0 copy-done.1
  173.0 0.0 copy-done.2
  173.0 6.2 %convolution_convert_fusion.1 = bf16[2048,1024]{1,0:T(8,128)(2,1)} fusion(bf16[1024,2048]{1,0:T(8,128)(2,1)S(1)} %copy-done.1, bf16[1024,1024]{1,0:T(8,128)(2,1)S(1)} %copy-done.2), kind=kOutput, calls=%fused_computation.1 | convolution fusion | flops 4297064448 | bytes 10485760 | tf_op jit(solution)/shard_map/dot_general | solution.py:1779
  179.2 35.8 %mixing.1 = (bf16[1024,2048]{1,0:T(8,128)(2,1)}, f32[1024,256]{1,0:T(8,128)}, f32[1024,128]{1,0:T(8,128)}, bf16[128,2048]{1,0:T(8,128)(2,1)}, bf16[4,64,1024]{2,1,0:T(8,128)(2,1)}) custom-call(bf16[1024,2048]{1,0:T(8,128)(2,1)} %get-tuple-element.78.refs_0_.refs_8_, bf16[1024,2048]{1,0:T(8,128)(2,1)} %get-tuple-element.79.refs_1_.refs_5_, ...), custom_call_target="tpu_custom_call" | custom-call | flops 15000000512 | bytes 60000000 | tf_op jit(solution)/shard_map/mixing/pallas_call | solution.py:1790
  215.0 51.8 %back.1 = (bf16[1024,2432]{1,0:T(8,128)(2,1)}, f32[8,2304]{1,0:T(8,128)}, f32[8,2304]{1,0:T(8,128)}, f32[8,2304]{1,0:T(8,128)}, f32[8,128]{1,0:T(8,128)}, /*index=5*/f32[64,1024]{1,0:T(8,128)}, f32[32,2048]{1,0:T(8,128)}) custom-call(f32[1,1]{1,0:T(1,128)} %bitcast.1.refs_4_.refs_0_, bf16[128,2048]{1,0:T(8,128)(2,1)} %get-tuple-element.83.refs_1_, ...), custom_call_target="tpu_custom_call" | custom-call | flops 15000000512 | bytes 60000000 | tf_op jit(solution)/shard_map/back/pallas_call | solution.py:1828
  266.8 48.1 %final.1 = (bf16[1024,1024]{1,0:T(8,128)(2,1)}, f32[32,4384]{1,0:T(8,128)}, f32[8,2304]{1,0:T(8,128)}, f32[1,1024]{1,0:T(1,128)}) custom-call(bf16[1024,1024]{1,0:T(8,128)(2,1)} %get-tuple-element.77.refs_0_, bf16[1024,2432]{1,0:T(8,128)(2,1)} %get-tuple-element.97.refs_1_.refs_3_, bf16[1024,2048]{1,0:T(8,128)(2,1)} %get-tuple-element.96.refs_2_, ...), custom_call_target="tpu_custom_call" | custom-call | flops 20000000000 | bytes 60000000 | tf_op jit(solution)/shard_map/final/pallas_call | solution.py:1481
  314.9 6.1 %close.1 = (f32[1024,1024]{1,0:T(8,128)}, f32[32,4384]{1,0:T(8,128)}, f32[64,1024]{1,0:T(8,128)}, f32[1024]{0:T(1024)}, f32[4,2304]{1,0:T(4,128)}, /*index=5*/f3...) custom-call(bf16[1024,1024]{1,0:T(8,128)(2,1)} %get-tuple-element.104.part_ref, ...), custom_call_target="tpu_custom_call" | custom-call | tf_op jit(solution)/shard_map/close/pallas_call | solution.py:1563
Async XLA Ops:
  41.8 61.5 %copy-start = (bf16[1040,1024]{1,0:T(8,128)(2,1)S(1)}, bf16[1040,1024]{1,0:T(8,128)(2,1)}, u32[]{:S(2)}) copy-start(bf16[1040,1024]{1,0:T(8,128)(2,1)} %get-tuple-element.65.refs_0_.refs_1_) | copy-start | bytes 6389764
  164.3 8.7 %copy-start.1 = (bf16[1024,2048]{1,0:T(8,128)(2,1)S(1)}, bf16[1024,2048]{1,0:T(8,128)(2,1)}, u32[]{:S(2)}) copy-start(bf16[1024,2048]{1,0:T(8,128)(2,1)} %get-tuple-element.81) | copy-start | bytes 12582916
  164.3 8.7 %copy-start.2 = (bf16[1024,1024]{1,0:T(8,128)(2,1)S(1)}, bf16[1024,1024]{1,0:T(8,128)(2,1)}, u32[]{:S(2)}) copy-start(bf16[1024,1024]{1,0:T(8,128)(2,1)} %get-tuple-element.82) | copy-start | bytes 6291460
